TPU v7x, 128 devices: a whole 4x4x4 slice. The times are simulated.
128 devices in a mesh: elem: 128 (over x, y, z, core).
Axes of the slice: x: 4, y: 4, z: 4, core: 2. Of those that a mesh axis runs over, the one named last changes fastest.
Arguments:
- tracer: float32 [1024, 8, 640], P('elem'), may hold values from 0 to 1
- old_mass: float32 [1024, 128], P('elem'), may hold values from 0.3 to 3
- new_mass: float32 [1024, 128], P('elem'), may hold values from 0.3 to 3
- dep_owner: int32 [1024, 128, 1], P('elem'), may hold values from 0 to 127, as said below
- dep_local: int32 [1024, 128], P('elem'), may hold values from 0 to 7
- dep_coord: float32 [2, 1024, 128], P(None, 'elem'), may hold values from -1 to 1
Outputs:
- new_tracer: float32 [1024, 8, 640], P('elem')
Inputs may be any that keep to these rules, and one draw needn't show every extreme that they name: `dep_owner`: the rows of one device name their own device or one of at most five other devices; no other device is named more than 32 times among them, and one other device is named exactly 32 times.
All inputs are finite; a program needn't handle non-finite values.
Results may differ from a plain program's by a relative error of at most 0.0003.
Values sent between devices are 32-bit elements; how exact they have to be, the bound alone decides.
No kernel may reach another device: no remote copies, remote signals or barrier semaphores. Data moves between devices by JAX's collectives and lax.ppermute only.
A program may use at most 64 MiB of HBM per device.

v0:
```python
import functools
import math

import jax
import jax.numpy as jnp
from jax import lax
from jax.sharding import Mesh
from jax.sharding import PartitionSpec as P

ELEM = ("elem_0", "elem_1", "elem_2", "elem_3")


GLL_NODES = (-1.0, -0.4472135954999579, 0.4472135954999579, 1.0)


def one_axis_at_a_time(shard, axes):
    return functools.reduce(lax.psum, axes, shard)


def one_axis(coord):
    columns = []
    for node_own in range(4):
        factor = jnp.ones_like(coord)
        for node_other in range(4):
            if node_other != node_own:
                factor = (
                    factor
                    * (coord - GLL_NODES[node_other])
                    / (GLL_NODES[node_own] - GLL_NODES[node_other])
                )
        columns.append(factor)
    return jnp.stack(columns, axis=-1)


def lagrange_weights(coord_a, coord_b):
    weights_a = one_axis(coord_a)
    weights_b = one_axis(coord_b)
    return (weights_a[..., :, None] * weights_b[..., None, :]).reshape(coord_a.shape + (16,))


def bound_terms(interp, lowest, highest):
    clipped = jnp.clip(interp, lowest, highest)
    margin = 0.01 + 0.05 * (highest - lowest)
    upper = highest + margin - clipped
    lower = clipped - lowest + margin
    return (clipped, upper, lower)


def fixer_terms(interp, lowest, highest, mass_new):
    clipped, upper, lower = bound_terms(interp, lowest, highest)
    sums = (
        jnp.sum(mass_new * clipped, axis=(0, 2)),
        jnp.sum(mass_new * upper, axis=(0, 2)),
        jnp.sum(mass_new * lower, axis=(0, 2)),
    )
    return (clipped, upper, lower, sums)


def apply_fix(clipped, upper, lower, source_total, clip_total, up_total, down_total):
    deficit = (source_total - clip_total)[:, None, :]
    return (
        clipped
        + jnp.maximum(deficit, 0.0) / up_total[:, None, :] * upper
        + jnp.minimum(deficit, 0.0) / down_total[:, None, :] * lower
    )


def body(tracer, old_mass, new_mass, dep_owner, dep_local, dep_coord):
    devices_count = lax.axis_size(ELEM)
    myself = lax.axis_index(ELEM)
    elems, levels, width = tracer.shape
    nodes = 16
    tracers = width // nodes
    total_rows = elems * levels * nodes
    capacity = total_rows // 32
    owner_flat = dep_owner.reshape(total_rows)
    is_home = owner_flat == myself
    level_index = jnp.broadcast_to(
        (jnp.arange(levels * nodes, dtype=jnp.int32) // nodes)[None, :], (elems, levels * nodes)
    ).reshape(total_rows)
    row_index = dep_local.reshape(total_rows) * levels + level_index
    peer_ids = jnp.arange(devices_count, dtype=jnp.int32)
    one_hot = (
        (owner_flat[:, None] == peer_ids[None, :]) & jnp.logical_not(is_home)[:, None]
    ).astype(jnp.int32)
    slot_index = jnp.sum(one_hot * (jnp.cumsum(one_hot, axis=0) - 1), axis=1)
    send_owner = jnp.where(is_home, devices_count, owner_flat)
    coord_a = dep_coord[0].reshape(total_rows)
    coord_b = dep_coord[1].reshape(total_rows)
    payload = jnp.stack([coord_a, coord_b], axis=-1)
    send_rows = (
        jnp.zeros((devices_count, capacity), jnp.int32)
        .at[send_owner, slot_index]
        .set(row_index, mode="drop")
    )
    send_load = (
        jnp.zeros((devices_count, capacity, payload.shape[-1]), jnp.float32)
        .at[send_owner, slot_index]
        .set(payload, mode="drop")
    )
    table_rows = elems * levels
    node_table = tracer.reshape(table_rows * nodes, tracers)
    per_node = tracer.reshape(table_rows, nodes, tracers)
    bounds_table = jnp.concatenate([jnp.min(per_node, axis=1), jnp.max(per_node, axis=1)], axis=-1)
    cell_ids = jnp.arange(table_rows, dtype=jnp.int32)
    shape4 = (elems, levels, nodes, tracers)
    mass_old = old_mass.reshape(elems, levels, nodes, 1)
    mass_new = new_mass.reshape(elems, levels, nodes, 1)
    local_source = jnp.sum(mass_old * tracer.reshape(shape4), axis=(0, 2))

    def evaluate_rows(rows, load):
        leading = rows.shape
        flat_rows = rows.reshape(-1)
        flat_load = load.reshape(-1, load.shape[-1])
        count = flat_rows.shape[0]
        weights = lagrange_weights(flat_load[:, 0], flat_load[:, 1])
        step_rows = math.gcd(count, 512)

        def one_block(inputs):
            block_rows, block_weights = inputs
            selector = (block_rows[:, None] == cell_ids[None, :]).astype(jnp.float32)
            spread = (selector[:, :, None] * block_weights[:, None, :]).reshape(
                step_rows, table_rows * nodes
            )
            values = jnp.dot(spread, node_table, precision=lax.Precision.HIGHEST)
            bounds = jnp.dot(selector, bounds_table, precision=lax.Precision.HIGHEST)
            return jnp.concatenate([values, bounds], axis=-1)

        blocks = lax.map(
            one_block,
            (
                flat_rows.reshape(count // step_rows, step_rows),
                weights.reshape(count // step_rows, step_rows, nodes),
            ),
        )
        return blocks.reshape(leading + (3 * tracers,))

    home_combined = evaluate_rows(row_index, payload)
    recv_rows = lax.all_to_all(send_rows, ELEM, split_axis=0, concat_axis=0, tiled=True)
    recv_load = lax.all_to_all(send_load, ELEM, split_axis=0, concat_axis=0, tiled=True)
    answers = lax.all_to_all(
        evaluate_rows(recv_rows, recv_load), ELEM, split_axis=0, concat_axis=0, tiled=True
    )
    combined = jnp.where(is_home[:, None], home_combined, answers[owner_flat, slot_index])
    interp = combined[:, :tracers].reshape(shape4)
    lowest = combined[:, tracers : 2 * tracers].reshape(shape4)
    highest = combined[:, 2 * tracers :].reshape(shape4)
    clipped, upper, lower, sums = fixer_terms(interp, lowest, highest, mass_new)
    source_total, clip_total, up_total, down_total = (
        one_axis_at_a_time(local_source, ELEM),
        one_axis_at_a_time(sums[0], ELEM),
        one_axis_at_a_time(sums[1], ELEM),
        one_axis_at_a_time(sums[2], ELEM),
    )
    result = apply_fix(clipped, upper, lower, source_total, clip_total, up_total, down_total)
    return result.reshape(elems, levels, width)


def solution(mesh):
    torus = Mesh(mesh.devices.reshape(4, 4, 4, 2), ("elem_0", "elem_1", "elem_2", "elem_3"))
    placed = (
        P(ELEM, None, None),
        P(ELEM, None),
        P(ELEM, None),
        P(ELEM, None, None),
        P(ELEM, None),
        P(None, ELEM, None),
    )
    return jax.shard_map(
        body, mesh=torus, in_specs=placed, out_specs=P(ELEM, None, None), check_vma=False
    )
```

profile of v0, /device:TPU:1, one launch (start us, length us, event | category | flops | bytes accessed | tf_op | source)
XLA Modules:
  0.0 159.5 jit_solution(16700626934893065508)
XLA Ops:
  0.1 0.9 copy.48
  1.0 0.7 compare_not_fusion
  1.8 0.3 fusion.15
  2.4 0.5 fusion.14
  3.2 4.3 %scatter_custom_fusion = s32[4096]{0:T(1024)S(1)} fusion(s32[1024]{0:T(1024)S(1)} %get-tuple-element.235, s32[1024]{0:T(1024)S(1)} %get-tuple-element.230, s32[]{:T(128)} %copy.81), kind=kCustom, calls=%fused_computation.68 | custom fusion | bytes 16388
  7.5 0.7 copy.51
  8.2 11.5 %all-to-all-start = ((s32[128,1,32]{2,1,0:T(1,128)}), s32[128,1,32]{2,1,0:T(1,128)S(1)}, u32[]{:S(2)}, u32[]{:S(2)}) async-start(s32[128,1,32]{2,1,0:T(1,128)} %copy.51), calls=%async_computation | async-start | bytes 131072 | tf_op jit(solution)/shard_map/all_to_all | solution.py:139
  19.8 0.4 reshape.520
  20.8 3.6 %scatter_custom_fusion.1 = f32[4096,2]{1,0:T(8,128)S(1)} fusion(s32[1024]{0:T(1024)S(1)} %get-tuple-element.234, f32[1024,2]{1,0:T(8,128)S(1)} %copy.52, f32[]{:T(128)} %constant.167.clone.1), kind=kCustom, calls=%fused_computation.25 | custom fusion | bytes 32772
  24.4 1.5 copy.53
  25.9 3.2 %all-to-all-done = s32[128,1,32]{2,1,0:T(1,128)S(1)} async-done(((s32[128,1,32]{2,1,0:T(1,128)}), s32[128,1,32]{2,1,0:T(1,128)S(1)}, u32[]{:S(2)}, u32[]{:S(2)}) %all-to-all-start) | async-done | bytes 16416 | tf_op jit(solution)/shard_map/all_to_all | solution.py:139
  29.1 6.5 %all-to-all-start.1 = ((f32[128,32,2]{1,2,0:T(2,128)}), f32[128,32,2]{1,2,0:T(2,128)S(1)}, u32[]{:S(2)}, u32[]{:S(2)}) async-start(f32[128,32,2]{1,2,0:T(2,128)} %copy.53), calls=%async_computation.1 | async-start | bytes 262144 | tf_op jit(solution)/shard_map/all_to_all | solution.py:140
  35.7 0.4 reshape.519
  36.2 0.6 broadcast.919
  36.8 0.8 reduce.12
  37.7 7.7 %all-to-all-done.1 = f32[128,32,2]{1,2,0:T(2,128)S(1)} async-done(((f32[128,32,2]{1,2,0:T(2,128)}), f32[128,32,2]{1,2,0:T(2,128)S(1)}, u32[]{:S(2)}, u32[]{:S(2)}) %all-to-all-start.1) | async-done | bytes 32800 | tf_op jit(solution)/shard_map/all_to_all | solution.py:140
  45.5 0.3 multiply_multiply_fusion.7
  46.2 17.6 %while.23 = (s32[]{:T(128)}, f32[8,512,120]{1,2,0:T(8,128)S(1)}, s32[8,512]{1,0:T(8,128)S(1)}, f32[8,512,16]{1,0,2:T(8,128)S(1)}, f32[1024,40]{1,0:T(8,128)S(1)}, /*index=5*/f32[64,80]{1,0:T(8,128)S(1)}, s32[]{:T(128)}) while((s32[]{:T(128)}, f32[8,512,120]{1,2,0:T(8,128)S(1)}, s32[8,512]{1,0:T(8,128)S(1)}, ...), condition=%wide.region_10.11_spmd.clone, body=%wide.region_9.10_spmd.clone.sunk | while | flops 283799552 | bytes 5550169 | solution.py:129
  46.3 0.3 broadcast_multiply_fusion.8
  46.5 1.5 fusion.65
  48.1 0.3 fusion.63
  48.5 0.3 broadcast_multiply_fusion.8
  48.7 1.5 fusion.65
  50.3 0.3 fusion.63
  50.7 0.3 broadcast_multiply_fusion.8
  50.9 1.5 fusion.65
  52.5 0.3 fusion.63
  52.9 0.3 broadcast_multiply_fusion.8
  53.1 1.5 fusion.65
  54.6 0.3 fusion.63
  55.1 0.3 broadcast_multiply_fusion.8
  55.3 1.5 fusion.65
  56.8 0.3 fusion.63
  57.3 0.3 broadcast_multiply_fusion.8
  57.5 1.5 fusion.65
  59.0 0.3 fusion.63
  59.5 0.3 broadcast_multiply_fusion.8
  59.7 1.5 fusion.65
  61.2 0.3 fusion.63
  61.7 0.3 broadcast_multiply_fusion.8
  61.9 1.5 fusion.65
  63.4 0.3 fusion.63
  63.8 1.9 %copy.56 = f32[8,512,120]{2,1,0:T(8,128)} copy(f32[8,512,120]{1,2,0:T(8,128)S(1)} %get-tuple-element.80) | data formatting | bytes 3932160 | tf_op jit(solution)/shard_map/while | solution.py:129
  65.6 4.5 %all-to-all-start.2 = ((f32[128,32,120]{2,1,0:T(8,128)}), f32[128,32,120]{2,1,0:T(8,128)S(1)}, u32[]{:S(2)}, u32[]{:S(2)}) async-start(f32[128,32,120]{2,1,0:T(8,128)} %bitcast.96), calls=%async_computation.2 | async-start | bytes 4194304 | tf_op jit(solution)/shard_map/all_to_all | solution.py:141
  70.2 4.4 %while.22 = (s32[]{:T(128)}, f32[2,512,120]{1,2,0:T(8,128)S(1)}, s32[2,512]{1,0:T(2,128)S(1)}, f32[2,512,16]{1,0,2:T(2,128)S(1)}, f32[1024,40]{1,0:T(8,128)S(1)}, /*index=5*/f32[64,80]{1,0:T(8,128)S(1)}, s32[]{:T(128)}) while((s32[]{:T(128)}, f32[2,512,120]{1,2,0:T(8,128)S(1)}, s32[2,512]{1,0:T(2,128)S(1)}, ...), condition=%wide.region_3.4_spmd.clone, body=%wide.region_2.3_spmd.clone.sunk | while | flops 283799552 | bytes 5550169 | solution.py:129
  70.3 0.3 broadcast_multiply_fusion.7
  70.6 1.5 fusion.58
  72.1 0.3 fusion.56
  72.5 0.3 broadcast_multiply_fusion.7
  72.8 1.5 fusion.58
  74.3 0.3 fusion.56
  75.2 0.9 mul.440
  76.1 0.9 multiply_reduce_fusion.3
  77.1 23.6 %all-to-all-done.2 = f32[128,32,120]{2,1,0:T(8,128)S(1)} async-done(((f32[128,32,120]{2,1,0:T(8,128)}), f32[128,32,120]{2,1,0:T(8,128)S(1)}, u32[]{:S(2)}, u32[]{:S(2)}) %all-to-all-start.2) | async-done | bytes 1966112 | tf_op jit(solution)/shard_map/all_to_all | solution.py:141
  100.7 6.8 %gather_fusion = f32[1024,120]{1,0:T(8,128)S(1)} fusion(f32[128,32,120]{2,1,0:T(8,128)S(1)} %all-to-all-done.2, s32[1024]{0:T(1024)S(1)} %bitcast.95), kind=kCustom, calls=%fused_computation | custom fusion | bytes 991232 | tf_op jit(solution)/shard_map/gather | solution.py:144
  107.7 0.3 fusion.29
  108.3 0.3 reshape.527
  108.6 0.3 reshape.528
  108.8 0.4 multiply_reduce_fusion.1
  109.2 11.6 %all-reduce.2 = (f32[8,40]{1,0:T(8,128)S(1)}, f32[8,40]{1,0:T(8,128)S(1)}, f32[8,40]{1,0:T(8,128)S(1)}, f32[8,40]{1,0:T(8,128)S(1)}) all-reduce(f32[8,40]{1,0:T(8,128)S(1)} %get-tuple-element.158, f32[8,40]{1,0:T(8,128)S(1)} %reduce_sum.58, ...), channel_id=1, replica_groups=mesh['elem_0'=4,'elem_1'=4,'elem_2'=4,'elem_3'=2] {'elem_0'}, use_global_device_ids=true, to_apply=%region_28.29 | all-reduce | flops 1280 | bytes 10240 | tf_op jit(solution)/shard_map/psum | solution.py:17
  120.8 11.0 %all-reduce.1 = (f32[8,40]{1,0:T(8,128)S(1)}, f32[8,40]{1,0:T(8,128)S(1)}, f32[8,40]{1,0:T(8,128)S(1)}, f32[8,40]{1,0:T(8,128)S(1)}) all-reduce(f32[8,40]{1,0:T(8,128)S(1)} %get-tuple-element.196, f32[8,40]{1,0:T(8,128)S(1)} %get-tuple-element.197, ...), channel_id=1, replica_groups=mesh['elem_0'=4,'elem_1'=4,'elem_2'=4,'elem_3'=2] {'elem_1'}, use_global_device_ids=true, to_apply=%region_29.30 | all-reduce | flops 1280 | bytes 10240 | tf_op jit(solution)/shard_map/psum | solution.py:17
  131.7 11.7 %all-reduce = (f32[8,40]{1,0:T(8,128)S(1)}, f32[8,40]{1,0:T(8,128)S(1)}, f32[8,40]{1,0:T(8,128)S(1)}, f32[8,40]{1,0:T(8,128)S(1)}) all-reduce(f32[8,40]{1,0:T(8,128)S(1)} %get-tuple-element.192, f32[8,40]{1,0:T(8,128)S(1)} %get-tuple-element.193, ...), channel_id=1, replica_groups=mesh['elem_0'=4,'elem_1'=4,'elem_2'=4,'elem_3'=2] {'elem_2'}, use_global_device_ids=true, to_apply=%region_30.31 | all-reduce | flops 1280 | bytes 10240 | tf_op jit(solution)/shard_map/psum | solution.py:17
  143.4 15.2 %all-reduce.3 = (f32[8,40]{1,0:T(8,128)S(1)}, f32[8,40]{1,0:T(8,128)S(1)}, f32[8,40]{1,0:T(8,128)S(1)}, f32[8,40]{1,0:T(8,128)S(1)}) all-reduce(f32[8,40]{1,0:T(8,128)S(1)} %get-tuple-element.188, f32[8,40]{1,0:T(8,128)S(1)} %get-tuple-element.189, ...), channel_id=1, replica_groups=mesh['elem_0'=4,'elem_1'=4,'elem_2'=4,'elem_3'=2] {'elem_3'}, use_global_device_ids=true, to_apply=%region_31.32 | all-reduce | flops 1280 | bytes 10240 | tf_op jit(solution)/shard_map/psum | solution.py:17
  158.8 0.7 multiply_add_fusion.1
  (117 shorter events, 4.0 us)
Async XLA Ops:
  0.0 2.9 %copy-start.9 = (s32[2]{0:T(128)S(1)}, s32[2]{0:T(128)}, u32[]{:S(2)}) copy-start(s32[2]{0:T(128)} %constant.198) | copy-start | bytes 28
  0.0 3.0 %copy-start.7 = (s32[2]{0:T(128)S(1)}, s32[2]{0:T(128)}, u32[]{:S(2)}) copy-start(s32[2]{0:T(128)} %constant.195) | copy-start | bytes 28
  0.0 3.0 %copy-start.8 = (s32[2]{0:T(128)S(1)}, s32[2]{0:T(128)}, u32[]{:S(2)}) copy-start(s32[2]{0:T(128)} %constant.201) | copy-start | bytes 28
  0.0 2.3 %copy-start.2 = (s32[8,128,1]{1,2,0:T(1,128)S(1)}, s32[8,128,1]{1,2,0:T(1,128)}, u32[]{:S(2)}) copy-start(s32[8,128,1]{1,2,0:T(1,128)} %param.13) | copy-start | bytes 12292
  0.0 3.1 %copy-start.4 = (s32[8,128]{1,0:T(8,128)S(1)}, s32[8,128]{1,0:T(8,128)}, u32[]{:S(2)}) copy-start(s32[8,128]{1,0:T(8,128)} %param.14) | copy-start | bytes 12292
  0.0 19.7 %copy-start.3 = (f32[2,8,128]{2,1,0:T(8,128)S(1)}, f32[2,8,128]{2,1,0:T(8,128)}, u32[]{:S(2)}) copy-start(f32[2,8,128]{2,1,0:T(8,128)} %param.15) | copy-start | bytes 24580
  0.0 19.7 %copy-start = (f32[8,8,640]{2,1,0:T(8,128)S(1)}, f32[8,8,640]{2,1,0:T(8,128)}, u32[]{:S(2)}) copy-start(f32[8,8,640]{2,1,0:T(8,128)} %param.10) | copy-start | bytes 491524
  8.2 20.9 %all-to-all-start = ((s32[128,1,32]{2,1,0:T(1,128)}), s32[128,1,32]{2,1,0:T(1,128)S(1)}, u32[]{:S(2)}, u32[]{:S(2)}) async-start(s32[128,1,32]{2,1,0:T(1,128)} %copy.51), calls=%async_computation | async-start | bytes 131072 | tf_op jit(solution)/shard_map/all_to_all | solution.py:139
  29.1 16.3 %all-to-all-start.1 = ((f32[128,32,2]{1,2,0:T(2,128)}), f32[128,32,2]{1,2,0:T(2,128)S(1)}, u32[]{:S(2)}, u32[]{:S(2)}) async-start(f32[128,32,2]{1,2,0:T(2,128)} %copy.53), calls=%async_computation.1 | async-start | bytes 262144 | tf_op jit(solution)/shard_map/all_to_all | solution.py:140
  65.6 4.5 %copy-start.1 = (f32[2,512,120]{1,2,0:T(8,128)S(1)}, f32[2,512,120]{1,2,0:T(8,128)}, u32[]{:S(2)}) copy-start(f32[2,512,120]{1,2,0:T(8,128)} %custom-call.2) | copy-start | bytes 1474564
  65.6 35.1 %all-to-all-start.2 = ((f32[128,32,120]{2,1,0:T(8,128)}), f32[128,32,120]{2,1,0:T(8,128)S(1)}, u32[]{:S(2)}, u32[]{:S(2)}) async-start(f32[128,32,120]{2,1,0:T(8,128)} %bitcast.96), calls=%async_computation.2 | async-start | bytes 4194304 | tf_op jit(solution)/shard_map/all_to_all | solution.py:141
  70.2 4.6 %copy-start.5 = (f32[8,128]{1,0:T(8,128)S(1)}, f32[8,128]{1,0:T(8,128)}, u32[]{:S(2)}) copy-start(f32[8,128]{1,0:T(8,128)} %param.12) | copy-start | bytes 12292
  70.2 4.7 %copy-start.6 = (f32[8,128]{1,0:T(8,128)S(1)}, f32[8,128]{1,0:T(8,128)}, u32[]{:S(2)}) copy-start(f32[8,128]{1,0:T(8,128)} %param.11) | copy-start | bytes 12292
where the time goes:
time: 160 us
  blocking collectives  49.4 us (31%)
  waiting for transfers between devices  34.5 us (22%)
  local copies, waits for them, and re-layouts  25.2 us (16%)
  starting transfers between devices  22.5 us (14%)
  matrix products  17.8 us (11%)
  other arithmetic  8.92 us (6%)
    psum x4, blocking collectives, one_axis_at_a_time(): return functools.reduce(lax.psum, axes, shard)  49.4 us
    all_to_all x1, waiting for transfers between devices, body(): lax.all_to_all(evaluate_rows(recv_rows, recv_load), ELEM, split_axis=0, c...  23.6 us
    dot_general x10, matrix products, one_block(): values = jnp.dot(spread, node_table, precision=lax.Precision.HIGHEST)  15.1 us
    all_to_all x1, starting transfers between devices, body(): lax.all_to_all(send_rows, ELEM, split_axis=0, concat_axis=0, tiled=True)  11.5 us
    unnamed x22, local copies, waits for them, and re-layouts  7.97 us
    all_to_all x1, waiting for transfers between devices, body(): lax.all_to_all(send_load, ELEM, split_axis=0, concat_axis=0, tiled=True)  7.67 us
    gather x1, local copies, waits for them, and re-layouts, body(): answers[owner_flat, slot_index]  6.78 us
    all_to_all x1, starting transfers between devices, body(): lax.all_to_all(send_load, ELEM, split_axis=0, concat_axis=0, tiled=True)  6.52 us
  transfers between devices with their start and end apart: 3, of which 3 were waited for; matrix products, arithmetic and copies ran while one was open for 9% of the time, Pallas kernels for 0%

commit v1 on v0

v1 whole, which is shorter than its diff:
```python
import jax
import jax.numpy as jnp
from jax import lax
from jax.experimental import pallas as pl
from jax.experimental.pallas import tpu as pltpu
from jax.sharding import PartitionSpec as P

GLL = (-1.0, -0.4472135954999579, 0.4472135954999579, 1.0)
DEVS = 128
ELEMS = 8
LEVELS = 8
NODES = 16
Q = 40
SLOTS = 32
COLS = LEVELS * NODES
F32, BF16, I32 = jnp.float32, jnp.bfloat16, jnp.int32
NT = (((1,), (1,)), ((), ()))


def iota(shape, dim):
    return lax.broadcasted_iota(I32, shape, dim)


def dot(a, b):
    return jnp.dot(a, b, preferred_element_type=F32)


def dot_nt(a, b):
    return lax.dot_general(a, b, NT, preferred_element_type=F32)


def split2(x):
    high = x.astype(BF16)
    return high, (x - high.astype(F32)).astype(BF16)


def split3(x):
    high = x.astype(BF16)
    rest = x - high.astype(F32)
    mid = rest.astype(BF16)
    return high, mid, (rest - mid.astype(F32)).astype(BF16)


def pack_kernel(me_ref, owner_ref, local_ref, coord_ref, mass_ref, req_ref, idx_ref, peer_ref):
    me = me_ref[0]
    sub = iota((DEVS, COLS), 0)
    lane = iota((DEVS, COLS), 1)
    level = (iota((1, COLS), 1) // NODES).astype(F32)
    before = jnp.where(sub < lane, 1.0, 0.0).astype(BF16)
    counter = jnp.concatenate([before, jnp.ones((COLS, COLS), BF16)], axis=1)
    owners, hots = [], []
    for e in range(ELEMS):
        owner = owner_ref[e : e + 1, :]
        owner = jnp.where(owner == me, -1, owner)
        owners.append(owner)
        hots.append(jnp.where(jnp.broadcast_to(owner, (DEVS, COLS)) == sub, 1.0, 0.0))
    counts = dot(jnp.concatenate(hots, axis=0).astype(BF16), counter)
    total = counts[:DEVS, COLS:]
    for e in range(1, ELEMS):
        total = total + counts[e * DEVS : (e + 1) * DEVS, COLS:]
    present = jnp.where(total > 0.0, 1.0, 0.0)
    earlier = jnp.where(lane < sub, 1.0, 0.0).astype(BF16)
    peer = dot(earlier, present.astype(BF16))
    base = peer * 0.0
    slot = sub % SLOTS
    wide = []
    for e in range(ELEMS):
        part = counts[e * DEVS : (e + 1) * DEVS]
        place = (part[:, :COLS] + base) * 8.0 + peer
        base = base + part[:, COLS:]
        row = jnp.sum(hots[e] * place, axis=0, keepdims=True)
        idx_ref[e : e + 1, :] = jnp.where(owners[e] >= 0, row, -1.0)
        rank = row.astype(I32) // 8
        local = local_ref[e : e + 1, :].astype(F32) * float(LEVELS) + level
        values = (local, coord_ref[0, e : e + 1, :], coord_ref[1, e : e + 1, :], mass_ref[e : e + 1, :])
        value = jnp.concatenate([jnp.broadcast_to(v, (SLOTS, COLS)) for v in values], axis=0)
        wide.append(jnp.where(jnp.broadcast_to(rank, (DEVS, COLS)) == slot, value, 0.0))
    hot = jnp.concatenate(hots, axis=1).astype(BF16)
    high, mid, low = split3(jnp.concatenate(wide, axis=1))
    req_ref[...] = dot_nt(hot, high) + dot_nt(hot, mid) + dot_nt(hot, low)
    ids = []
    owner_id = sub.astype(F32)
    for p in range(8):
        mine = jnp.where(peer == float(p), present, 0.0)
        ids.append(jnp.sum(mine * owner_id, axis=0, keepdims=True))
    peer_ref[...] = jnp.concatenate(ids, axis=0).astype(I32)


def node_constants(n):
    def one(index):
        p0 = jnp.where(index > 0, GLL[0], GLL[1])
        p1 = jnp.where(index > 1, GLL[1], GLL[2])
        p2 = jnp.where(index > 2, GLL[2], GLL[3])
        scale = []
        for i in range(4):
            prod = 1.0
            for j in range(4):
                if j != i:
                    prod *= GLL[i] - GLL[j]
            scale.append(1.0 / prod)
        c = jnp.where(index == 0, scale[0], jnp.where(index == 1, scale[1], jnp.where(index == 2, scale[2], scale[3])))
        return p0, p1, p2, c

    k = iota((NODES, n), 0)
    return one(k // 4), one(k % 4)


def lagrange(x, consts):
    p0, p1, p2, c = consts
    return ((x - p0) * (x - p1)) * ((x - p2) * c)


def evaluate(row, a, b, mass, table, bounds, consts):
    n = row.shape[1]
    index = row.astype(I32)
    index8 = jnp.broadcast_to(index, (8, n))
    elem8 = index8 // LEVELS
    level8 = index8 % LEVELS
    w = lagrange(jnp.broadcast_to(a, (NODES, n)), consts[0]) * lagrange(jnp.broadcast_to(b, (NODES, n)), consts[1])
    wh = w.astype(BF16).astype(F32)
    wm = w - wh
    sh, sm = [], []
    for e in range(ELEMS):
        here = elem8 == e
        for h in range(2):
            sh.append(jnp.where(here, wh[8 * h : 8 * h + 8], 0.0))
            sm.append(jnp.where(here, wm[8 * h : 8 * h + 8], 0.0))
    sh = jnp.concatenate(sh, axis=0).astype(BF16)
    sm = jnp.concatenate(sm, axis=0).astype(BF16)
    r = dot(table, jnp.concatenate([sh, sm, sh], axis=0))
    hot = []
    sub8 = iota((8, n), 0)
    for e in range(ELEMS):
        hot.append(jnp.where(index8 == sub8 + 8 * e, 1.0, 0.0))
    hot = jnp.concatenate(hot, axis=0).astype(BF16)
    lim = dot(bounds, jnp.concatenate([hot, hot, hot], axis=0))
    at = [level8 == l for l in range(LEVELS)]
    clipped, highest, lowest = [], [], []
    for t in range(Q // 8):
        v = r[8 * t : 8 * t + 8]
        for l in range(1, LEVELS):
            v = jnp.where(at[l], r[l * Q + 8 * t : l * Q + 8 * t + 8], v)
        lo = lim[8 * t : 8 * t + 8]
        hi = lim[Q + 8 * t : Q + 8 * t + 8]
        clipped.append(jnp.minimum(jnp.maximum(v, lo), hi))
        highest.append(hi)
        lowest.append(lo)
    mass8 = jnp.broadcast_to(mass, (8, n))
    mh = mass8.astype(BF16).astype(F32)
    mm = mass8 - mh
    mine = level8 == sub8
    by_level = jnp.concatenate([jnp.where(mine, mh, 0.0), jnp.where(mine, mm, 0.0)], axis=0).astype(BF16)
    ch, cm = split2(jnp.concatenate(clipped, axis=0))
    sums = dot_nt(jnp.concatenate([ch, cm], axis=0), by_level)
    mmh = mm.astype(BF16).astype(F32)
    mass3 = jnp.where(sub8 == 0, mh, jnp.where(sub8 == 1, mmh, jnp.where(sub8 == 2, mm - mmh, 0.0)))
    hist = dot_nt(jnp.concatenate([mass3, mass3 * 0.0], axis=0).astype(BF16), hot)
    return clipped, highest, lowest, sums, hist


def spread_terms(clipped, highest, lowest):
    margin = 0.01 + 0.05 * (highest - lowest)
    return highest + margin - clipped, clipped - lowest + margin


def level_sums(sums, hist, low_table, high_table):
    s = sums[:Q] + sums[Q:]
    clip = s[:, :LEVELS] + s[:, LEVELS:]
    mass = hist[0:1] + hist[1:2] + hist[2:3]

    def fold(x):
        total = x[:, :LEVELS]
        for e in range(1, ELEMS):
            total = total + x[:, e * LEVELS : (e + 1) * LEVELS]
        return total

    s_low = fold(low_table * mass)
    s_high = fold(high_table * mass)
    margin = 0.01 * fold(jnp.broadcast_to(mass, (Q, mass.shape[1]))) + 0.05 * (s_high - s_low)
    return clip, s_high + margin - clip, clip - s_low + margin


def home_kernel(me_ref, t_ref, old_ref, owner_ref, local_ref, coord_ref, mass_ref, bt_ref, table_ref, bounds_ref, part_ref, c_ref, up_ref, down_ref):
    me = me_ref[0]
    t = t_ref[...]
    th, tm = split2(t)
    table = jnp.concatenate([th, th, tm], axis=1)
    table_ref[...] = table
    bh, bm, bl = split3(bt_ref[...])
    bounds = jnp.concatenate([bh, bm, bl], axis=1)
    bounds_ref[...] = bounds
    lane = iota((Q, COLS), 1)
    source = jnp.zeros((Q, COLS), F32)
    for l in range(LEVELS):
        s = jnp.sum(t[l * Q : (l + 1) * Q] * old_ref[l : l + 1, :], axis=1, keepdims=True)
        source = jnp.where(lane == l, s, source)
    level = iota((1, COLS), 1) // NODES
    n = 2 * COLS
    consts = node_constants(n)
    sums, hist = None, None
    for e in range(0, ELEMS, 2):

        def pair(f):
            return jnp.concatenate([f(e), f(e + 1)], axis=1)

        row = pair(lambda i: (local_ref[i : i + 1, :] * LEVELS + level).astype(F32))
        a = pair(lambda i: coord_ref[0, i : i + 1, :])
        b = pair(lambda i: coord_ref[1, i : i + 1, :])
        mass = pair(lambda i: jnp.where(owner_ref[i : i + 1, :] == me, mass_ref[i : i + 1, :], 0.0))
        clipped, highest, lowest, s, h = evaluate(row, a, b, mass, table, bounds, consts)
        sums = s if sums is None else sums + s
        hist = h if hist is None else hist + h
        for i in range(Q // 8):
            up, down = spread_terms(clipped[i], highest[i], lowest[i])
            for j in range(2):
                at = slice((e + j) * Q + 8 * i, (e + j) * Q + 8 * i + 8)
                c_ref[at, :] = clipped[i][:, j * COLS : (j + 1) * COLS]
                up_ref[at, :] = up[:, j * COLS : (j + 1) * COLS]
                down_ref[at, :] = down[:, j * COLS : (j + 1) * COLS]
    clip, up, down = level_sums(sums, hist, bt_ref[:Q, :], bt_ref[Q:, :])
    pad = jnp.zeros((Q, COLS - 3 * LEVELS), F32)
    part_ref[...] = jnp.concatenate([source[:, :LEVELS] - clip, up, down, pad], axis=1)


def serve_kernel(req_ref, table_ref, bounds_ref, part_ref, bt_ref, sums_ref, level_ref, c_ref, up_ref, down_ref):
    rows = req_ref[...].T
    level_ref[...] = (rows[:SLOTS].astype(I32) % LEVELS).astype(F32)
    table = table_ref[...]
    bounds = bounds_ref[...]
    consts = node_constants(2 * DEVS)
    sums, hist = None, None
    for s0 in range(0, SLOTS, 2):

        def pair(v):
            return jnp.concatenate([rows[v * SLOTS + s0 : v * SLOTS + s0 + 1], rows[v * SLOTS + s0 + 1 : v * SLOTS + s0 + 2]], axis=1)

        clipped, highest, lowest, s, h = evaluate(pair(0), pair(1), pair(2), pair(3), table, bounds, consts)
        sums = s if sums is None else sums + s
        hist = h if hist is None else hist + h
        for i in range(Q // 8):
            up, down = spread_terms(clipped[i], highest[i], lowest[i])
            for j in range(2):
                at = slice((s0 + j) * Q + 8 * i, (s0 + j) * Q + 8 * i + 8)
                c_ref[at, :] = clipped[i][:, j * DEVS : (j + 1) * DEVS]
                up_ref[at, :] = up[:, j * DEVS : (j + 1) * DEVS]
                down_ref[at, :] = down[:, j * DEVS : (j + 1) * DEVS]
    clip, up, down = level_sums(sums, hist, bt_ref[:Q, :], bt_ref[Q:, :])
    part = jnp.concatenate([-clip, up, down], axis=1) + part_ref[:, : 3 * LEVELS]
    packed = [part[8 * i : 8 * i + 8] for i in range(Q // 8)]
    packed.append(jnp.zeros((8, COLS - 3 * LEVELS * (Q // 8)), F32))
    packed = jnp.concatenate(packed, axis=1)
    for d in range(DEVS):
        sums_ref[8 * d : 8 * d + 8, :] = packed


def finish_kernel(tot_ref, level_ref, c_ref, up_ref, down_ref, ans_ref, home_ref, out_scratch):
    total = tot_ref[0:8, :]
    for d in range(1, DEVS):
        total = total + tot_ref[8 * d : 8 * d + 8, :]
    up_total = pltpu.roll(total, COLS - LEVELS, 1)
    down_total = pltpu.roll(total, COLS - 2 * LEVELS, 1)
    rise = jnp.maximum(total, 0.0) / up_total
    fall = jnp.minimum(total, 0.0) / down_total
    home_level = iota((8, COLS), 1) // NODES
    for i in range(Q // 8):
        rises = [jnp.broadcast_to(rise[:, 24 * i + l : 24 * i + l + 1], (8, DEVS)) for l in range(LEVELS)]
        falls = [jnp.broadcast_to(fall[:, 24 * i + l : 24 * i + l + 1], (8, DEVS)) for l in range(LEVELS)]
        hr, hf = rises[0], falls[0]
        for l in range(1, LEVELS):
            hr = jnp.where(home_level == l, rises[l], hr)
            hf = jnp.where(home_level == l, falls[l], hf)
        home_ref[8 * i : 8 * i + 8, :] = hr
        home_ref[Q + 8 * i : Q + 8 * i + 8, :] = hf
        for s in range(SLOTS):
            level8 = jnp.broadcast_to(level_ref[s : s + 1, :].astype(I32), (8, DEVS))
            r, f = rises[0], falls[0]
            for l in range(1, LEVELS):
                r = jnp.where(level8 == l, rises[l], r)
                f = jnp.where(level8 == l, falls[l], f)
            at = slice(s * Q + 8 * i, s * Q + 8 * i + 8)
            out_scratch[at, :] = c_ref[at, :] + r * up_ref[at, :] + f * down_ref[at, :]
    for j in range(SLOTS * Q // 128):
        ans_ref[pl.ds(j, DEVS, stride=SLOTS * Q // 128), :] = out_scratch[128 * j : 128 * (j + 1), :].T


def place_kernel(idx_ref, hot_ref, scratch):
    cols = jnp.concatenate([idx_ref[...], jnp.full((COLS - ELEMS, COLS), -1.0, F32)], axis=0).T
    scratch[...] = cols
    turned = jnp.concatenate([scratch[pl.ds(k, LEVELS, stride=NODES), :] for k in range(NODES)], axis=0)
    lane = iota((COLS, SLOTS * 8), 1).astype(F32)
    for e in range(ELEMS):
        col = jnp.broadcast_to(turned[:, e : e + 1], (COLS, SLOTS * 8))
        hot_ref[e * COLS : (e + 1) * COLS, :] = jnp.where(col == lane, 1.0, 0.0).astype(BF16)


def home_finish_kernel(coef_ref, idx_ref, c_ref, up_ref, down_ref, out_ref, scratch):
    for e in range(ELEMS):
        at = slice(e * Q, (e + 1) * Q)
        v = c_ref[at, :] + coef_ref[:Q, :] * up_ref[at, :] + coef_ref[Q:, :] * down_ref[at, :]
        v = jnp.where(jnp.broadcast_to(idx_ref[e : e + 1, :], (Q, COLS)) < 0.0, v, 0.0)
        scratch[e] = jnp.concatenate([v, jnp.zeros((COLS - Q, COLS), F32)], axis=0).T
        for k in range(NODES):
            out_ref[e * COLS + 8 * k : e * COLS + 8 * k + 8, :] = scratch[e, pl.ds(k, LEVELS, stride=NODES), :]


def join_kernel(peer_ref, ans_ref, hot_ref, home_ref, out_ref, rows, sem):
    chunk = SLOTS * Q // 128
    copies = [
        pltpu.make_async_copy(ans_ref.at[pl.ds(peer_ref[p, 0] * chunk, chunk), :], rows.at[pl.ds(p * chunk, chunk), :], sem.at[p])
        for p in range(5)
    ]
    for copy in copies:
        copy.start()
    rows[5 * chunk :, :] = jnp.zeros((3 * chunk, 128), F32)
    for copy in copies:
        copy.wait()
    flat = jnp.concatenate([rows[pl.ds(j, 8, stride=chunk), :] for j in range(chunk)], axis=1)
    table = jnp.concatenate([flat[:, s * Q : (s + 1) * Q] for s in range(SLOTS)], axis=0)
    high, mid = split2(table)
    for e in range(ELEMS):
        hot = hot_ref[e * COLS : (e + 1) * COLS, :]
        v = dot(hot, high) + dot(hot, mid) + home_ref[e * COLS : (e + 1) * COLS, :Q]
        out_ref[e] = jnp.concatenate([v[8 * k : 8 * k + 8] for k in range(NODES)], axis=1)


def body(tracer, old_mass, new_mass, dep_owner, dep_local, dep_coord):
    me = lax.axis_index("elem").astype(I32).reshape(1)
    owner = dep_owner.reshape(ELEMS, COLS)
    vmem = pl.BlockSpec(memory_space=pltpu.VMEM)
    smem = pl.BlockSpec(memory_space=pltpu.SMEM)

    def shape(rows, cols, dtype=F32):
        return jax.ShapeDtypeStruct((rows, cols), dtype)

    def exchange(x, chunk):
        y = lax.all_to_all(x.reshape((DEVS,) + chunk), "elem", 0, 0, tiled=True)
        return y.reshape(x.shape)

    req, idx, peer = pl.pallas_call(
        pack_kernel,
        out_shape=(shape(DEVS, COLS), shape(ELEMS, COLS), shape(8, COLS, I32)),
        in_specs=[smem] + [vmem] * 4,
        out_specs=(vmem,) * 3,
        name="pack",
    )(me, owner, dep_local, dep_coord, new_mass)
    asked = exchange(req, (1, COLS))

    nodes = tracer.reshape(ELEMS, LEVELS, NODES, Q)
    t = jnp.transpose(nodes, (1, 3, 0, 2)).reshape(LEVELS * Q, ELEMS * NODES)
    old = jnp.transpose(old_mass.reshape(ELEMS, LEVELS, NODES), (1, 0, 2)).reshape(LEVELS, COLS)
    bt = jnp.concatenate([jnp.min(nodes, axis=2), jnp.max(nodes, axis=2)], axis=-1).reshape(ELEMS * LEVELS, 2 * Q).T
    table, bounds, part, hc, hu, hd = pl.pallas_call(
        home_kernel,
        out_shape=(shape(LEVELS * Q, 3 * COLS, BF16), shape(2 * Q, 3 * ELEMS * LEVELS, BF16), shape(Q, COLS))
        + (shape(ELEMS * Q, COLS),) * 3,
        in_specs=[smem] + [vmem] * 7,
        out_specs=(vmem,) * 6,
        name="home",
    )(me, t, old, owner, dep_local, dep_coord, new_mass, bt)

    sums, level, c, up, down = pl.pallas_call(
        serve_kernel,
        out_shape=(shape(8 * DEVS, COLS), shape(SLOTS, DEVS)) + (shape(SLOTS * Q, DEVS),) * 3,
        in_specs=[vmem] * 5,
        out_specs=(vmem,) * 5,
        name="serve",
    )(asked, table, bounds, part, bt)
    totals = exchange(sums, (8, COLS))

    hot = pl.pallas_call(
        place_kernel,
        out_shape=shape(ELEMS * COLS, SLOTS * 8, BF16),
        in_specs=[vmem],
        out_specs=vmem,
        scratch_shapes=[pltpu.VMEM((COLS, COLS), F32)],
        name="place",
    )(idx)

    ans, coef = pl.pallas_call(
        finish_kernel,
        out_shape=(shape(SLOTS * Q * DEVS // 128, 128), shape(2 * Q, COLS)),
        in_specs=[vmem] * 5,
        out_specs=(vmem,) * 2,
        scratch_shapes=[pltpu.VMEM((SLOTS * Q, DEVS), F32)],
        name="finish",
    )(totals, level, c, up, down)
    got = exchange(ans, (1, SLOTS * Q))

    home = pl.pallas_call(
        home_finish_kernel,
        out_shape=shape(ELEMS * COLS, 128),
        in_specs=[vmem] * 5,
        out_specs=vmem,
        scratch_shapes=[pltpu.VMEM((ELEMS, COLS, 128), F32)],
        name="home_finish",
    )(coef, idx, hc, hu, hd)

    return pl.pallas_call(
        join_kernel,
        out_shape=jax.ShapeDtypeStruct((ELEMS, LEVELS, NODES * Q), F32),
        in_specs=[smem, pl.BlockSpec(memory_space=pl.ANY), vmem, vmem],
        out_specs=vmem,
        scratch_shapes=[pltpu.VMEM((8 * SLOTS * Q // 128, 128), F32), pltpu.SemaphoreType.DMA((5,))],
        name="join",
    )(peer, got, hot, home)


def solution(mesh):
    placed = (
        P("elem", None, None),
        P("elem", None),
        P("elem", None),
        P("elem", None, None),
        P("elem", None),
        P(None, "elem", None),
    )
    return jax.shard_map(body, mesh=mesh, in_specs=placed, out_specs=P("elem", None, None), check_vma=False)
```

time: 160 us -> 78.3 us (0.49)
  blocking collectives: 49.4 us -> 20.1 us
  Pallas kernels: 0 us -> 22.5 us
  local copies, waits for them, and re-layouts: 25.2 us -> 4.41 us
  waiting for transfers between devices: 34.5 us -> 14.4 us
  matrix products: 17.8 us -> 0 us
  other arithmetic: 8.92 us -> 0.29 us
  starting transfers between devices: 22.5 us -> 16.2 us
    psum x4 -> x0, blocking collectives: 49.4 us -> none  [one_axis_at_a_time(): return functools.reduce(lax.psum, axes, shard)]
    pallas_call x0 -> x7, Pallas kernels: none -> 22.5 us  [the longest x1 6.39 us: body(): pl.pallas_call(serve_kernel, out_shape=(shape(8 * DEVS, COLS), shape(SLOT...]
    all_to_all x3 -> x2, waiting for transfers between devices: 34.5 us -> 14.4 us  [exchange(): y = lax.all_to_all(x.reshape((DEVS,) + chunk), 'elem', 0, 0, tiled=True)]
    all_to_all x0 -> x1, blocking collectives: none -> 20.1 us  [exchange(): y = lax.all_to_all(x.reshape((DEVS,) + chunk), 'elem', 0, 0, tiled=True)]
    dot_general x20 -> x0, matrix products: 17.8 us -> none  [the longest x10 15.1 us: one_block(): values = jnp.dot(spread, node_table, precision=lax.Precision.HIGHEST)]
    gather x1 -> x0, local copies, waits for them, and re-layouts: 6.78 us -> none  [body(): answers[owner_flat, slot_index]]
    unnamed x22 -> x8, local copies, waits for them, and re-layouts: 7.97 us -> 1.48 us
    all_to_all x3 -> x2, starting transfers between devices: 22.5 us -> 16.2 us  [exchange(): y = lax.all_to_all(x.reshape((DEVS,) + chunk), 'elem', 0, 0, tiled=True)]
  transfers between devices with their start and end apart: 3 -> 2, of which waited for: 3 -> 2; matrix products, arithmetic and copies ran while one was open for 9% -> 4% of each run, Pallas kernels for 0% -> 9%
where the time goes in v1:
time: 78.3 us; the launch traced here: 77.9 us
  Pallas kernels  22.5 us (29%)
  blocking collectives  20.1 us (26%)
  starting transfers between devices  16.2 us (21%)
  waiting for transfers between devices  14.4 us (18%)
  local copies, waits for them, and re-layouts  4.41 us (6%)
    all_to_all x1, blocking collectives, exchange(): y = lax.all_to_all(x.reshape((DEVS,) + chunk), 'elem', 0, 0, tiled=True)  20.1 us
    all_to_all x2, starting transfers between devices, exchange(): y = lax.all_to_all(x.reshape((DEVS,) + chunk), 'elem', 0, 0, tiled=True)  16.2 us
    all_to_all x2, waiting for transfers between devices, exchange(): y = lax.all_to_all(x.reshape((DEVS,) + chunk), 'elem', 0, 0, tiled=True)  14.4 us
    pallas_call x1, Pallas kernels, body(): pl.pallas_call(serve_kernel, out_shape=(shape(8 * DEVS, COLS), shape(SLOT...  6.39 us
    pallas_call x1, Pallas kernels, body(): pl.pallas_call(finish_kernel, out_shape=(shape(SLOTS * Q * DEVS // 128, 1...  3.37 us
    pallas_call x1, Pallas kernels, body(): pl.pallas_call(join_kernel, out_shape=jax.ShapeDtypeStruct((ELEMS, LEVELS...  3.26 us
    pallas_call x1, Pallas kernels, body(): pl.pallas_call(home_kernel, out_shape=(shape(LEVELS * Q, 3 * COLS, BF16),...  2.77 us
    pallas_call x1, Pallas kernels, body(): pl.pallas_call(pack_kernel, out_shape=(shape(DEVS, COLS), shape(ELEMS, CO...  2.63 us
  transfers between devices with their start and end apart: 2, of which 2 were waited for; matrix products, arithmetic and copies ran while one was open for 4% of the time, Pallas kernels for 9%

profile of v1, /device:TPU:1, one launch (start us, length us, event | category | flops | bytes accessed | tf_op | source)
XLA Modules:
  0.0 77.9 jit_solution(13298612283526955267)
XLA Ops:
  0.0 0.0 copy-start.2
  0.0 2.6 %pack.1 = (f32[128,128]{1,0:T(8,128)}, f32[8,128]{1,0:T(8,128)}, s32[8,128]{1,0:T(8,128)}) custom-call(s32[1]{0:T(128)} %bitcast.me_ref, s32[8,128]{1,0:T(8,128)} %bitcast.33, s32[8,128]{1,0:T(8,128)} %local_ref.3, f32[2,8,128]{2,1,0:T(8,128)} %coord_ref.3, f32[8,128]{1,0:T(8,128)} %mass_ref.3), custom_call_target="tpu_custom_call" | custom-call | tf_op jit(solution)/shard_map/pack/pallas_call | solution.py:339
  2.6 11.5 %all-to-all-start = ((f32[128,1,128]{2,1,0:T(1,128)}), f32[128,1,128]{2,1,0:T(1,128)S(1)}, u32[]{:S(2)}, u32[]{:S(2)}) async-start(f32[128,1,128]{2,1,0:T(1,128)} %bitcast.32), calls=%async_computation | async-start | bytes 131072 | tf_op jit(solution)/shard_map/all_to_all | solution.py:336
  14.1 0.0 copy-done.2
  14.1 0.4 reshape.43
  14.5 0.2 fusion
  14.7 0.2 copy.21
  14.9 0.1 maximum_bitcast_fusion
  15.0 0.7 copy.16
  15.7 0.2 reshape.44
  15.9 0.0 copy-start.3
  15.9 0.8 %copy.17.t_ref = f32[320,128]{1,0:T(8,128)} copy(f32[320,128]{0,1:T(8,128)S(1)} %reshape.44) | data formatting | bytes 327680 | tf_op jit(solution)/shard_map/reshape | solution.py:349
  16.7 0.0 copy-done.3
  16.7 0.1 reshape.45
  16.7 0.7 reshape.46.old_ref
  17.4 2.8 %home.1 = (bf16[320,384]{1,0:T(8,128)(2,1)}, bf16[80,192]{1,0:T(8,128)(2,1)}, f32[40,128]{1,0:T(8,128)}, f32[320,128]{1,0:T(8,128)}, f32[320,128]{1,0:T(8,128)}, /*index=5*/f32[320,128]{1,0:T(8,128)}) custom-call(s32[1]{0:T(128)} %bitcast.me_ref, f32[320,128]{1,0:T(8,128)} %copy.17.t_ref, f32[8,128]{1,0:T(8,128)} %reshape.46.old_ref, s32[8,128]{1,0:T(8,128)} %bitcast.34, ...), custom_call_target="tpu_custom_call" | custom-call | tf_op jit(solution)/shard_map/home/pallas_call | solution.py:352
  20.2 3.3 %all-to-all-done = f32[128,1,128]{2,1,0:T(1,128)S(1)} async-done(((f32[128,1,128]{2,1,0:T(1,128)}), f32[128,1,128]{2,1,0:T(1,128)S(1)}, u32[]{:S(2)}, u32[]{:S(2)}) %all-to-all-start) | async-done | bytes 65568 | tf_op jit(solution)/shard_map/all_to_all | solution.py:336
  23.5 0.0 copy-start.1
  23.5 0.6 copy-done.1
  24.1 6.4 %serve.1 = (f32[1024,128]{1,0:T(8,128)}, f32[32,128]{1,0:T(8,128)}, f32[1280,128]{1,0:T(8,128)}, f32[1280,128]{1,0:T(8,128)}, f32[1280,128]{1,0:T(8,128)}) custom-call(f32[128,128]{1,0:T(8,128)} %bitcast.30, bf16[320,384]{1,0:T(8,128)(2,1)} %get-tuple-element.23.table_ref, bf16[80,192]{1,0:T(8,128)(2,1)} %get-tuple-element.24.bounds_ref, ...), custom_call_target="tpu_custom_call" | custom-call | tf_op jit(solution)/shard_map/serve/pallas_call | solution.py:361
  30.5 20.1 %all_to_all.15 = f32[128,8,128]{2,1,0:T(8,128)} all-to-all(f32[128,8,128]{2,1,0:T(8,128)} %bitcast.27), channel_id=1, replica_groups=mesh['elem'=128] {'elem'}, dimensions={0} | all-to-all | bytes 1048576 | tf_op jit(solution)/shard_map/all_to_all | solution.py:336
  50.6 3.4 %finish.1 = (f32[1280,128]{1,0:T(8,128)}, f32[80,128]{1,0:T(8,128)}) custom-call(f32[1024,128]{1,0:T(8,128)} %bitcast.24, f32[32,128]{1,0:T(8,128)} %get-tuple-element.27.level_ref, f32[1280,128]{1,0:T(8,128)} %get-tuple-element.28.c_ref, f32[1280,128]{1,0:T(8,128)} %get-tuple-element.29.up_ref, f32[1280,128]{1,0:T(8,128)} %get-tuple-element.30.down_ref), custom_call_target="tpu_custom_call" | custom-call | tf_op jit(solution)/shard_map/finish/pallas_call | solution.py:379
  54.0 4.7 %all-to-all-start.2 = ((f32[128,1,1280]{2,1,0:T(1,128)}), f32[128,1,1280]{2,1,0:T(1,128)S(1)}, u32[]{:S(2)}, u32[]{:S(2)}) async-start(f32[128,1,1280]{2,1,0:T(1,128)} %bitcast.26), calls=%async_computation.2 | async-start | bytes 1310720 | tf_op jit(solution)/shard_map/all_to_all | solution.py:336
  58.7 1.8 %place.1.hot_ref = bf16[1024,256]{1,0:T(8,128)(2,1)} custom-call(f32[8,128]{1,0:T(8,128)} %get-tuple-element.32.idx_ref), custom_call_target="tpu_custom_call" | custom-call | tf_op jit(solution)/shard_map/place/pallas_call | solution.py:370
  60.5 2.2 %home_finish.1.home_ref = f32[1024,128]{1,0:T(8,128)} custom-call(f32[80,128]{1,0:T(8,128)} %get-tuple-element.33.coef_ref, f32[8,128]{1,0:T(8,128)} %get-tuple-element.32.idx_ref, f32[320,128]{1,0:T(8,128)} %get-tuple-element.34.c_ref, f32[320,128]{1,0:T(8,128)} %get-tuple-element.35.up_ref, f32[320,128]{1,0:T(8,128)} %get-tuple-element.36.down_ref), custom_call_target="tpu_custom_call" | custom-call | tf_op jit(solution)/shard_map/home_finish/pallas_call | solution.py:389
  62.8 11.0 %all-to-all-done.2 = f32[128,1,1280]{2,1,0:T(1,128)S(1)} async-done(((f32[128,1,1280]{2,1,0:T(1,128)}), f32[128,1,1280]{2,1,0:T(1,128)S(1)}, u32[]{:S(2)}, u32[]{:S(2)}) %all-to-all-start.2) | async-done | bytes 655392 | tf_op jit(solution)/shard_map/all_to_all | solution.py:336
  73.8 0.0 copy-start
  73.8 0.8 %copy-done = f32[128,1,1280]{2,1,0:T(1,128)} copy-done((f32[128,1,1280]{2,1,0:T(1,128)}, f32[128,1,1280]{2,1,0:T(1,128)S(1)}, u32[]{:S(2)}) %copy-start) | copy-done | bytes 655384
  74.6 3.3 %join.1 = f32[8,8,640]{2,1,0:T(8,128)} custom-call(s32[8,128]{1,0:T(8,128)} %get-tuple-element.21.peer_ref, f32[1280,128]{1,0:T(8,128)} %bitcast.23, bf16[1024,256]{1,0:T(8,128)(2,1)} %place.1.hot_ref, f32[1024,128]{1,0:T(8,128)} %home_finish.1.home_ref), custom_call_target="tpu_custom_call" | custom-call | tf_op jit(solution)/shard_map/join/pallas_call | solution.py:398
  (1 shorter events, 0.0 us)
Async XLA Ops:
  0.0 14.1 %copy-start.2 = (f32[8,8,640]{2,1,0:T(8,128)S(1)}, f32[8,8,640]{2,1,0:T(8,128)}, u32[]{:S(2)}) copy-start(f32[8,8,640]{2,1,0:T(8,128)} %param.6) | copy-start | bytes 491524
  2.6 20.9 %all-to-all-start = ((f32[128,1,128]{2,1,0:T(1,128)}), f32[128,1,128]{2,1,0:T(1,128)S(1)}, u32[]{:S(2)}, u32[]{:S(2)}) async-start(f32[128,1,128]{2,1,0:T(1,128)} %bitcast.32), calls=%async_computation | async-start | bytes 131072 | tf_op jit(solution)/shard_map/all_to_all | solution.py:336
  15.9 0.8 %copy-start.3 = (f32[8,128]{1,0:T(8,128)S(1)}, f32[8,128]{1,0:T(8,128)}, u32[]{:S(2)}) copy-start(f32[8,128]{1,0:T(8,128)} %param.7) | copy-start | bytes 12292
  23.5 0.6 copy-start.1
  54.0 19.8 %all-to-all-start.2 = ((f32[128,1,1280]{2,1,0:T(1,128)}), f32[128,1,1280]{2,1,0:T(1,128)S(1)}, u32[]{:S(2)}, u32[]{:S(2)}) async-start(f32[128,1,1280]{2,1,0:T(1,128)} %bitcast.26), calls=%async_computation.2 | async-start | bytes 1310720 | tf_op jit(solution)/shard_map/all_to_all | solution.py:336
  73.8 0.8 %copy-start = (f32[128,1,1280]{2,1,0:T(1,128)}, f32[128,1,1280]{2,1,0:T(1,128)S(1)}, u32[]{:S(2)}) copy-start(f32[128,1,1280]{2,1,0:T(1,128)S(1)} %all-to-all-done.2) | copy-start | bytes 1966084

commit v2 on v1

v2 whole, which is shorter than its diff:
```python
import jax
import jax.numpy as jnp
from jax import lax
from jax.experimental import pallas as pl
from jax.experimental.pallas import tpu as pltpu
from jax.sharding import PartitionSpec as P

GLL = (-1.0, -0.4472135954999579, 0.4472135954999579, 1.0)
DEVS = 128
ELEMS = 8
LEVELS = 8
NODES = 16
Q = 40
SLOTS = 32
PEERS = 5
COLS = LEVELS * NODES
CHUNK = SLOTS * Q // 128
F32, BF16, I32 = jnp.float32, jnp.bfloat16, jnp.int32
NT = (((1,), (1,)), ((), ()))


def iota(shape, dim):
    return lax.broadcasted_iota(I32, shape, dim)


def dot(a, b):
    return jnp.dot(a, b, preferred_element_type=F32)


def dot_nt(a, b):
    return lax.dot_general(a, b, NT, preferred_element_type=F32)


def split2(x):
    high = x.astype(BF16)
    return high, (x - high.astype(F32)).astype(BF16)


def split3(x):
    high = x.astype(BF16)
    rest = x - high.astype(F32)
    mid = rest.astype(BF16)
    return high, mid, (rest - mid.astype(F32)).astype(BF16)


def pack_kernel(me_ref, owner_hbm, local_hbm, coord_hbm, mass_hbm, old_hbm, tracer_hbm, req_ref, idx_ref, peer_ref, vals_ref, old_ref, tracer_ref, owner_ref, local_ref, coord_ref, mass_ref, sem):
    pairs = (
        (owner_hbm, owner_ref),
        (local_hbm, local_ref),
        (coord_hbm, coord_ref),
        (mass_hbm, mass_ref),
        (old_hbm, old_ref),
        (tracer_hbm, tracer_ref),
    )
    copies = [pltpu.make_async_copy(src, dst, sem.at[i]) for i, (src, dst) in enumerate(pairs)]
    for copy in copies:
        copy.start()
    me = me_ref[0]
    sub = iota((DEVS, COLS), 0)
    lane = iota((DEVS, COLS), 1)
    before = jnp.where(sub < lane, 1.0, 0.0).astype(BF16)
    counter = jnp.concatenate([before, jnp.ones((COLS, COLS), BF16)], axis=1)
    earlier = jnp.where(lane < sub, 1.0, 0.0).astype(BF16)
    for copy in copies[:4]:
        copy.wait()
    owner = owner_ref[...]
    away = owner != me
    owner = jnp.where(away, owner, -1)
    level = iota((ELEMS, COLS), 1) // NODES
    row = (local_ref[...] * LEVELS + (level + 1)).astype(F32)
    mass = mass_ref[...]
    vals_ref[:ELEMS] = row
    vals_ref[ELEMS : 2 * ELEMS] = coord_ref[0]
    vals_ref[2 * ELEMS : 3 * ELEMS] = coord_ref[1]
    vals_ref[3 * ELEMS :] = jnp.where(away, 0.0, mass)
    values = (row, coord_ref[0], coord_ref[1], mass)
    hots = [jnp.where(jnp.broadcast_to(owner[e : e + 1], (DEVS, COLS)) == sub, 1.0, 0.0) for e in range(ELEMS)]
    counts = dot(jnp.concatenate(hots, axis=0).astype(BF16), counter)
    total = counts[:DEVS, COLS:]
    for e in range(1, ELEMS):
        total = total + counts[e * DEVS : (e + 1) * DEVS, COLS:]
    present = jnp.where(total > 0.0, 1.0, 0.0)
    peer = dot(earlier, present.astype(BF16))
    base = peer * float(SLOTS)
    slot = sub % SLOTS
    wide, places = [], []
    for e in range(ELEMS):
        part = counts[e * DEVS : (e + 1) * DEVS]
        place = part[:, :COLS] + base
        base = base + part[:, COLS:]
        spot = jnp.sum(hots[e] * place, axis=0, keepdims=True).astype(I32)
        places.append(spot)
        value = jnp.concatenate([jnp.broadcast_to(v[e : e + 1], (SLOTS, COLS)) for v in values], axis=0)
        wide.append(jnp.where(jnp.broadcast_to(spot % SLOTS, (DEVS, COLS)) == slot, value, 0.0))
    idx_ref[...] = jnp.where(away, jnp.concatenate(places, axis=0), -1).astype(F32)
    hot = jnp.concatenate(hots, axis=1).astype(BF16)
    high, mid = split2(jnp.concatenate(wide, axis=1))
    req_ref[...] = dot_nt(hot, high) + dot_nt(hot, mid)
    owner_id = sub.astype(F32)
    ids = [jnp.sum(jnp.where(peer == float(p), present, 0.0) * owner_id, axis=0, keepdims=True) for p in range(PEERS)]
    named = jnp.sum(present, axis=0, keepdims=True)
    ids = [ids[0]] + [jnp.where(named > float(p), ids[p], ids[0]) for p in range(1, PEERS)]
    peer_ref[...] = jnp.concatenate(ids + [named] * (8 - PEERS), axis=0).astype(I32)
    for copy in copies[4:]:
        copy.wait()


def node_constants(n):
    def one(index):
        p0 = jnp.where(index > 0, GLL[0], GLL[1])
        p1 = jnp.where(index > 1, GLL[1], GLL[2])
        p2 = jnp.where(index > 2, GLL[2], GLL[3])
        scale = []
        for i in range(4):
            prod = 1.0
            for j in range(4):
                if j != i:
                    prod *= GLL[i] - GLL[j]
            scale.append(1.0 / prod)
        c = jnp.where(index == 0, scale[0], jnp.where(index == 1, scale[1], jnp.where(index == 2, scale[2], scale[3])))
        return p0, p1, p2, c

    k = iota((NODES, n), 0)
    return one(k // 4), one(k % 4)


def lagrange(x, consts):
    p0, p1, p2, c = consts
    return ((x - p0) * (x - p1)) * ((x - p2) * c)


def evaluate(row, a, b, mass, table, consts):
    n = row.shape[1]
    index = jnp.maximum(row.astype(I32) - 1, 0)
    index8 = jnp.broadcast_to(index, (8, n))
    level8 = index8 % LEVELS
    sub8 = iota((8, n), 0)
    hot = jnp.concatenate([jnp.where(index8 == sub8 + 8 * e, 1.0, 0.0) for e in range(ELEMS)], axis=0).astype(BF16)
    values = dot(table, jnp.concatenate([hot, hot, hot], axis=0))
    w = lagrange(jnp.broadcast_to(a, (NODES, n)), consts[0]) * lagrange(jnp.broadcast_to(b, (NODES, n)), consts[1])
    weights = [jnp.broadcast_to(w[k : k + 1], (8, n)) for k in range(NODES)]
    clipped, highest, lowest = [], [], []
    for t in range(Q // 8):
        v = values[8 * t : 8 * t + 8]
        total, low, high = weights[0] * v, v, v
        for k in range(1, NODES):
            v = values[k * Q + 8 * t : k * Q + 8 * t + 8]
            total = total + weights[k] * v
            low = jnp.minimum(low, v)
            high = jnp.maximum(high, v)
        clipped.append(jnp.minimum(jnp.maximum(total, low), high))
        highest.append(high)
        lowest.append(low)
    mass8 = jnp.broadcast_to(mass, (8, n))
    mh = mass8.astype(BF16).astype(F32)
    mm = mass8 - mh
    mine = level8 == sub8
    by_level = jnp.concatenate([jnp.where(mine, mh, 0.0), jnp.where(mine, mm, 0.0)], axis=0).astype(BF16)
    ch, cm = split2(jnp.concatenate(clipped, axis=0))
    sums = dot_nt(jnp.concatenate([ch, cm], axis=0), by_level)
    mmh = mm.astype(BF16).astype(F32)
    mass3 = jnp.where(sub8 == 0, mh, jnp.where(sub8 == 1, mmh, jnp.where(sub8 == 2, mm - mmh, 0.0)))
    hist = dot_nt(jnp.concatenate([mass3, mass3 * 0.0], axis=0).astype(BF16), hot)
    return clipped, highest, lowest, sums, hist, level8


def spread_terms(clipped, highest, lowest):
    margin = 0.01 + 0.05 * (highest - lowest)
    return highest + margin - clipped, clipped - lowest + margin


def fold(x):
    total = x[:, :LEVELS]
    for e in range(1, ELEMS):
        total = total + x[:, e * LEVELS : (e + 1) * LEVELS]
    return total


def level_sums(sums, hist, low_table, high_table):
    s = sums[:Q] + sums[Q:]
    clip = s[:, :LEVELS] + s[:, LEVELS:]
    mass = hist[0:1] + hist[1:2] + hist[2:3]

    s_low = fold(low_table * mass)
    s_high = fold(high_table * mass)
    margin = 0.01 * fold(jnp.broadcast_to(mass, (Q, mass.shape[1]))) + 0.05 * (s_high - s_low)
    return clip, s_high + margin - clip, clip - s_low + margin


def home_kernel(tracer_ref, old_ref, vals_ref, idx_ref, table_ref, bt_ref, part_ref, hot_ref, c_ref, up_ref, down_ref, scratch):
    rows = ELEMS * LEVELS
    node = iota((NODES, COLS), 0)
    column = iota((NODES, COLS), 1)
    wide = jnp.concatenate([jnp.where(column % NODES == node, jnp.broadcast_to(old_ref[e : e + 1, :], (NODES, COLS)), 0.0) for e in range(ELEMS)], axis=1)
    source_of = iota((ELEMS * COLS, rows), 0)
    gather = jnp.where(source_of // NODES == iota((ELEMS * COLS, rows), 1), 1.0, 0.0).astype(BF16)
    old = sum(dot(part, gather) for part in split3(wide))
    natural = tracer_ref[...].reshape(rows, NODES * Q)
    flat = [natural[:, 128 * j : 128 * (j + 1)].T for j in range(NODES * Q // 128)]
    for j, piece in enumerate(flat):
        table_ref[128 * j : 128 * (j + 1), :] = jnp.concatenate(split3(piece), axis=1)
    flat = jnp.concatenate(flat, axis=0)
    source = low = high = None
    for k in range(NODES):
        v = flat[k * Q : (k + 1) * Q]
        term = v * old[k : k + 1, :]
        source = term if source is None else source + term
        low = v if low is None else jnp.minimum(low, v)
        high = v if high is None else jnp.maximum(high, v)
    bt_ref[:Q] = low
    bt_ref[Q:] = high
    consts = node_constants(2 * COLS)
    table = table_ref[...]
    sums, hist = None, None
    for e in range(0, ELEMS, 2):
        args = [jnp.concatenate([vals_ref[v * ELEMS + e : v * ELEMS + e + 1], vals_ref[v * ELEMS + e + 1 : v * ELEMS + e + 2]], axis=1) for v in range(4)]
        clipped, highest, lowest, s, h, _ = evaluate(*args, table, consts)
        sums = s if sums is None else sums + s
        hist = h if hist is None else hist + h
        for i in range(Q // 8):
            up, down = spread_terms(clipped[i], highest[i], lowest[i])
            for j in range(2):
                at = slice((e + j) * Q + 8 * i, (e + j) * Q + 8 * i + 8)
                c_ref[at, :] = clipped[i][:, j * COLS : (j + 1) * COLS]
                up_ref[at, :] = up[:, j * COLS : (j + 1) * COLS]
                down_ref[at, :] = down[:, j * COLS : (j + 1) * COLS]
    clip, up, down = level_sums(sums, hist, low, high)
    pad = jnp.zeros((Q, COLS - 3 * LEVELS), F32)
    part_ref[...] = jnp.concatenate([fold(source) - clip, up, down, pad], axis=1)
    scratch[...] = jnp.concatenate([idx_ref[...], jnp.full((COLS - ELEMS, COLS), -1.0, F32)], axis=0).T
    turned = jnp.concatenate([scratch[pl.ds(k, LEVELS, stride=NODES), :] for k in range(NODES)], axis=0)
    lane = iota((COLS, SLOTS * 8), 1).astype(F32)
    for e in range(ELEMS):
        col = jnp.broadcast_to(turned[:, e : e + 1], (COLS, SLOTS * 8))
        hot_ref[e * COLS : (e + 1) * COLS, :] = jnp.where(col == lane, 1.0, 0.0).astype(BF16)


def serve_kernel(me_ref, req_ref, table_ref, part_ref, bt_ref, sums_ref, ids_ref, level_ref, c_ref, up_ref, down_ref, dense, tiles):
    req = req_ref[...]
    sub = iota((DEVS, DEVS), 0)
    lane = iota((DEVS, DEVS), 1)
    high, mid = split2(req)
    first = jnp.where(iota((16, DEVS), 1) == 0, 1.0, 0.0).astype(BF16)
    asks = jnp.where(dot_nt(first, high) > 0.0, 1.0, 0.0)
    place = dot(asks.astype(BF16), jnp.where(sub < lane, 1.0, 0.0).astype(BF16))
    count = jnp.sum(asks[0:1]).astype(I32)
    pick = jnp.where(jnp.broadcast_to(place[0:1], (DEVS, DEVS)) == sub.astype(F32), jnp.broadcast_to(asks[0:1], (DEVS, DEVS)), 0.0).astype(BF16)
    dense[...] = dot(pick, high) + dot(pick, mid)
    ids = dot_nt(iota((16, DEVS), 1).astype(F32).astype(BF16), pick)[:8].astype(I32)
    ids = jnp.where(iota((8, DEVS), 1) < count, ids, me_ref[0])
    ids_ref[...] = jnp.where(iota((8, DEVS), 0) == 0, ids, count)
    groups = [dense[pl.ds(i, DEVS // 4, stride=4), :] for i in range(4)]
    block = iota((DEVS // 4, DEVS), 1) // SLOTS
    for v in range(4):
        tile = None
        for i in range(4):
            shift = (i - v) * SLOTS % DEVS
            moved = pltpu.roll(groups[i], shift, 1) if shift else groups[i]
            tile = moved if tile is None else jnp.where(block == i, moved, tile)
        tiles[v] = tile
    consts = node_constants(2 * DEVS)

    def step(u, carry):
        args = [jnp.concatenate([tiles[v, pl.ds(2 * u, 1), :], tiles[v, pl.ds(2 * u + 1, 1), :]], axis=1) for v in range(4)]
        clipped, highest, lowest, s, h, level8 = evaluate(*args, table_ref[...], consts)
        for j in range(2):
            level_ref[pl.ds(pl.multiple_of(16 * u + 8 * j, 8), 8), :] = level8[:, j * DEVS : (j + 1) * DEVS]
        for i in range(Q // 8):
            up, down = spread_terms(clipped[i], highest[i], lowest[i])
            for j in range(2):
                at = pl.ds(pl.multiple_of(2 * Q * u + j * Q + 8 * i, 8), 8)
                c_ref[at, :] = clipped[i][:, j * DEVS : (j + 1) * DEVS]
                up_ref[at, :] = up[:, j * DEVS : (j + 1) * DEVS]
                down_ref[at, :] = down[:, j * DEVS : (j + 1) * DEVS]
        return carry[0] + s, carry[1] + h

    start = (jnp.zeros((2 * Q, 2 * LEVELS), F32), jnp.zeros((16, ELEMS * LEVELS), F32))
    sums, hist = lax.fori_loop(0, (count + 7) // 8, step, start)
    clip, up, down = level_sums(sums, hist, bt_ref[:Q, :], bt_ref[Q:, :])
    part = jnp.concatenate([-clip, up, down], axis=1) + part_ref[:, : 3 * LEVELS]
    packed = [part[8 * i : 8 * i + 8] for i in range(Q // 8)]
    packed.append(jnp.zeros((8, COLS - 3 * LEVELS * (Q // 8)), F32))
    packed = jnp.concatenate(packed, axis=1)
    for d in range(DEVS):
        sums_ref[8 * d : 8 * d + 8, :] = packed


def finish_kernel(ids_ref, tot_ref, level_ref, c_ref, up_ref, down_ref, idx_ref, hc_ref, hu_ref, hd_ref, ans_ref, home_ref, rises, falls, scratch):
    total = tot_ref[0:8, :]
    for d in range(1, DEVS):
        total = total + tot_ref[8 * d : 8 * d + 8, :]
    up_total = pltpu.roll(total, COLS - LEVELS, 1)
    down_total = pltpu.roll(total, COLS - 2 * LEVELS, 1)
    rise = jnp.maximum(total, 0.0) / up_total
    fall = jnp.minimum(total, 0.0) / down_total
    home_level = iota((8, COLS), 1) // NODES
    home_rise, home_fall = [], []
    for i in range(Q // 8):
        hr = hf = None
        for l in range(LEVELS):
            r = jnp.broadcast_to(rise[:, 24 * i + l : 24 * i + l + 1], (8, DEVS))
            f = jnp.broadcast_to(fall[:, 24 * i + l : 24 * i + l + 1], (8, DEVS))
            rises[i, l] = r
            falls[i, l] = f
            hr = r if hr is None else jnp.where(home_level == l, r, hr)
            hf = f if hf is None else jnp.where(home_level == l, f, hf)
        home_rise.append(hr)
        home_fall.append(hf)
    home_rise = jnp.concatenate(home_rise, axis=0)
    home_fall = jnp.concatenate(home_fall, axis=0)
    block = iota((CHUNK, DEVS), 1) // SLOTS

    def step(t, carry):
        level8 = level_ref[pl.ds(pl.multiple_of(8 * t, 8), 8), :]
        at_level = [level8 == l for l in range(LEVELS)]
        out = []
        for i in range(Q // 8):
            r, f = rises[i, 0], falls[i, 0]
            for l in range(1, LEVELS):
                r = jnp.where(at_level[l], rises[i, l], r)
                f = jnp.where(at_level[l], falls[i, l], f)
            at = pl.ds(pl.multiple_of(Q * t + 8 * i, 8), 8)
            out.append(c_ref[at, :] + r * up_ref[at, :] + f * down_ref[at, :])
        out = jnp.concatenate(out, axis=0)
        parts = [out[CHUNK * b : CHUNK * (b + 1)] for b in range(4)]
        for i in range(4):
            chunk = None
            for b in range(4):
                shift = (b - i) * SLOTS % DEVS
                moved = pltpu.roll(parts[b], shift, 1) if shift else parts[b]
                chunk = moved if chunk is None else jnp.where(block == b, moved, chunk)
            ans_ref[pl.ds(ids_ref[0, 4 * t + i] * CHUNK, CHUNK), :] = chunk
        return carry

    lax.fori_loop(0, (ids_ref[1, 0] + 3) // 4, step, 0)
    for e in range(ELEMS):
        at = slice(e * Q, (e + 1) * Q)
        v = hc_ref[at, :] + home_rise * hu_ref[at, :] + home_fall * hd_ref[at, :]
        v = jnp.where(jnp.broadcast_to(idx_ref[e : e + 1, :], (Q, COLS)) < 0.0, v, 0.0)
        scratch[e] = jnp.concatenate([v, jnp.zeros((COLS - Q, COLS), F32)], axis=0).T
        for k in range(NODES):
            home_ref[e * COLS + 8 * k : e * COLS + 8 * k + 8, :] = scratch[e, pl.ds(k, LEVELS, stride=NODES), :]


def join_kernel(peer_ref, ans_ref, hot_ref, home_ref, out_hbm, out_ref, sem):
    block = iota((CHUNK, 128), 1) // SLOTS
    chunks = [ans_ref[pl.ds(peer_ref[p, 0] * CHUNK, CHUNK), :] for p in range(PEERS)]
    table = []
    for b in range(4):

        def moved(p):
            shift = (p - b) * SLOTS % 128
            return pltpu.roll(chunks[p], shift, 1) if shift else chunks[p]

        near = moved(0)
        for p in range(1, 4):
            near = jnp.where(block == p, moved(p), near)
        table.append(jnp.concatenate([near, jnp.where(block == 0, moved(4), 0.0)], axis=1))
    high, mid = split2(jnp.concatenate(table, axis=0))
    for e in range(ELEMS):
        hot = hot_ref[e * COLS : (e + 1) * COLS, :]
        v = dot_nt(hot, high) + dot_nt(hot, mid) + home_ref[e * COLS : (e + 1) * COLS, :Q]
        out_ref[e] = jnp.concatenate([v[8 * k : 8 * k + 8] for k in range(NODES)], axis=1)
        pltpu.make_async_copy(out_ref.at[e], out_hbm.at[e], sem.at[e]).start()
    for e in range(ELEMS):
        pltpu.make_async_copy(out_ref.at[e], out_hbm.at[e], sem.at[e]).wait()


def body(tracer, old_mass, new_mass, dep_owner, dep_local, dep_coord):
    me = lax.axis_index("elem").astype(I32).reshape(1)
    owner = dep_owner.reshape(ELEMS, COLS)
    smem, vmem, hbm = (pl.BlockSpec(memory_space=m) for m in (pltpu.SMEM, pltpu.VMEM, pltpu.HBM))

    def near(*arrays):
        return [pltpu.with_memory_space_constraint(x, pltpu.VMEM) for x in arrays]

    def call(kernel, name, outs, in_specs, scratch, args):
        return pl.pallas_call(
            kernel,
            out_shape=tuple(pltpu.VMEM(shape, dtype) for shape, dtype in outs),
            in_specs=in_specs,
            out_specs=(vmem,) * len(outs),
            scratch_shapes=scratch,
            compiler_params=pltpu.CompilerParams(vmem_limit_bytes=20 << 20),
            name=name,
        )(*args)

    def exchange(x, chunk):
        y = lax.all_to_all(x.reshape((DEVS,) + chunk), "elem", 0, 0, tiled=True)
        return y.reshape(x.shape)

    req, idx, peer, vals, old, table_in = call(
        pack_kernel,
        "pack",
        (
            ((DEVS, COLS), F32),
            ((ELEMS, COLS), F32),
            ((8, COLS), I32),
            ((4 * ELEMS, COLS), F32),
            ((ELEMS, COLS), F32),
            (tracer.shape, F32),
        ),
        [smem] + [hbm] * 6,
        [
            pltpu.VMEM((ELEMS, COLS), I32),
            pltpu.VMEM((ELEMS, COLS), I32),
            pltpu.VMEM((2, ELEMS, COLS), F32),
            pltpu.VMEM((ELEMS, COLS), F32),
            pltpu.SemaphoreType.DMA((6,)),
        ],
        [me] + [pltpu.with_memory_space_constraint(x, pltpu.HBM) for x in (owner, dep_local, dep_coord, new_mass, old_mass, tracer)],
    )
    asked = exchange(req, (1, COLS))
    table, bt, part, hot, hc, hu, hd = call(
        home_kernel,
        "home",
        (
            ((NODES * Q, 3 * ELEMS * LEVELS), BF16),
            ((2 * Q, ELEMS * LEVELS), F32),
            ((Q, COLS), F32),
            ((ELEMS * COLS, SLOTS * 8), BF16),
        )
        + (((ELEMS * Q, COLS), F32),) * 3,
        [vmem] * 4,
        [pltpu.VMEM((COLS, COLS), F32)],
        near(table_in, old, vals, idx),
    )
    sums, ids, level, c, up, down = call(
        serve_kernel,
        "serve",
        (((8 * DEVS, COLS), F32), ((8, DEVS), I32), ((2 * DEVS, DEVS), I32)) + (((SLOTS * Q, DEVS), F32),) * 3,
        [smem] + [vmem] * 4,
        [pltpu.VMEM((DEVS, DEVS), F32), pltpu.VMEM((4, DEVS // 4, DEVS), F32)],
        [me] + near(asked, table, part, bt),
    )
    totals = exchange(sums, (8, COLS))
    ans, home = call(
        finish_kernel,
        "finish",
        (((DEVS * CHUNK, 128), F32), ((ELEMS * COLS, 128), F32)),
        [smem] + [vmem] * 9,
        [pltpu.VMEM((Q // 8, LEVELS, 8, DEVS), F32)] * 2 + [pltpu.VMEM((ELEMS, COLS, 128), F32)],
        [ids] + near(totals, level, c, up, down, idx, hc, hu, hd),
    )
    got = exchange(ans, (1, SLOTS * Q))
    return pl.pallas_call(
        join_kernel,
        out_shape=jax.ShapeDtypeStruct((ELEMS, LEVELS, NODES * Q), F32),
        in_specs=[smem] + [vmem] * 3,
        out_specs=hbm,
        scratch_shapes=[pltpu.VMEM((ELEMS, LEVELS, NODES * Q), F32), pltpu.SemaphoreType.DMA((ELEMS,))],
        compiler_params=pltpu.CompilerParams(vmem_limit_bytes=20 << 20),
        name="join",
    )(peer, *near(got, hot, home))


def solution(mesh):
    placed = (
        P("elem", None, None),
        P("elem", None),
        P("elem", None),
        P("elem", None, None),
        P("elem", None),
        P(None, "elem", None),
    )
    return jax.shard_map(body, mesh=mesh, in_specs=placed, out_specs=P("elem", None, None), check_vma=False)
```

time: 78.3 us -> 65.8 us (0.84)
  blocking collectives: 20.1 us -> 37.6 us
  Pallas kernels: 22.5 us -> 8.91 us
  waiting for transfers between devices: 14.4 us -> 7.55 us
  starting transfers between devices: 16.2 us -> 11.5 us
  local copies, waits for them, and re-layouts: 4.41 us -> 0 us
    all_to_all x1 -> x2, blocking collectives: 20.1 us -> 37.6 us  [exchange(): y = lax.all_to_all(x.reshape((DEVS,) + chunk), 'elem', 0, 0, tiled=True)]
    pallas_call x6 -> x4, Pallas kernels: 19.2 us -> 7.05 us  [call(): pl.pallas_call(kernel, out_shape=tuple((pltpu.VMEM(shape, dtype) for shap...]
    all_to_all x2 -> x1, waiting for transfers between devices: 14.4 us -> 7.55 us  [exchange(): y = lax.all_to_all(x.reshape((DEVS,) + chunk), 'elem', 0, 0, tiled=True)]
    all_to_all x2 -> x1, starting transfers between devices: 16.2 us -> 11.5 us  [exchange(): y = lax.all_to_all(x.reshape((DEVS,) + chunk), 'elem', 0, 0, tiled=True)]
    reshape x8 -> x0, local copies, waits for them, and re-layouts: 2.93 us -> none  [the longest x2 0.97 us: body(): t = jnp.transpose(nodes, (1, 3, 0, 2)).reshape(LEVELS * Q, ELEMS * NODES)]
    unnamed x8 -> x0, local copies, waits for them, and re-layouts: 1.48 us -> none
    pallas_call x1, Pallas kernels: 3.26 us -> 1.86 us  [body(): pl.pallas_call(join_kernel, out_shape=jax.ShapeDtypeStruct((ELEMS, LEVELS...]
  transfers between devices with their start and end apart: 2 -> 1, of which waited for: 2 -> 1; matrix products, arithmetic and copies ran while one was open for 4% -> 0% of each run, Pallas kernels for 9% -> 3%
where the time goes in v2:
time: 65.8 us; the launch traced here: 65.6 us
  blocking collectives  37.6 us (57%)
  starting transfers between devices  11.5 us (17%)
  Pallas kernels  8.91 us (14%)
  waiting for transfers between devices  7.55 us (11%)
    all_to_all x2, blocking collectives, exchange(): y = lax.all_to_all(x.reshape((DEVS,) + chunk), 'elem', 0, 0, tiled=True)  37.6 us
    all_to_all x1, starting transfers between devices, exchange(): y = lax.all_to_all(x.reshape((DEVS,) + chunk), 'elem', 0, 0, tiled=True)  11.5 us
    all_to_all x1, waiting for transfers between devices, exchange(): y = lax.all_to_all(x.reshape((DEVS,) + chunk), 'elem', 0, 0, tiled=True)  7.55 us
    pallas_call x4, Pallas kernels, call(): pl.pallas_call(kernel, out_shape=tuple((pltpu.VMEM(shape, dtype) for shap...  7.05 us
    pallas_call x1, Pallas kernels, body(): pl.pallas_call(join_kernel, out_shape=jax.ShapeDtypeStruct((ELEMS, LEVELS...  1.86 us
  transfers between devices with their start and end apart: 1, of which 1 were waited for; matrix products, arithmetic and copies ran while one was open for 0% of the time, Pallas kernels for 3%

profile of v2, /device:TPU:1, one launch (start us, length us, event | category | flops | bytes accessed | tf_op | source)
XLA Modules:
  0.0 65.6 jit_solution(14941636222331979384)
XLA Ops:
  0.0 2.5 %pack.1 = (f32[128,128]{1,0:T(8,128)}, f32[8,128]{1,0:T(8,128)S(1)}, s32[8,128]{1,0:T(8,128)S(1)}, f32[32,128]{1,0:T(8,128)S(1)}, f32[8,128]{1,0:T(8,128)S(1)}, /*index=5*/f32[8,8,640]{2,1,0:T(8,128)S(1)}) custom-call(s32[1]{0:T(128)} %bitcast.me_ref, s32[8,128]{1,0:T(8,128)} %bitcast.15, s32[8,128]{1,0:T(8,128)} %local_hbm.1, f32[2,8,128]{2,1,0:T(8,128)} %coord_hbm.1, ...), custom_call_target="tpu_custom_call" | custom-call | tf_op jit(solution)/shard_map/pack/pallas_call | solution.py:378
  2.5 11.5 %all-to-all-start = ((f32[128,1,128]{2,1,0:T(1,128)}), f32[128,1,128]{2,1,0:T(1,128)S(1)}, u32[]{:S(2)}, u32[]{:S(2)}) async-start(f32[128,1,128]{2,1,0:T(1,128)} %bitcast.3), calls=%async_computation | async-start | bytes 131072 | tf_op jit(solution)/shard_map/all_to_all | solution.py:389
  14.0 1.7 %home.1 = (bf16[640,192]{1,0:T(8,128)(2,1)S(1)}, f32[80,64]{1,0:T(8,128)S(1)}, f32[40,128]{1,0:T(8,128)S(1)}, bf16[1024,256]{1,0:T(8,128)(2,1)S(1)}, f32[320,128...) custom-call(f32[8,8,640]{2,1,0:T(8,128)S(1)} %get-tuple-element.28.tracer_ref, ...), custom_call_target="tpu_custom_call" | custom-call | tf_op jit(solution)/shard_map/home/pallas_call | solution.py:378
  15.8 7.6 %all-to-all-done = f32[128,1,128]{2,1,0:T(1,128)S(1)} async-done(((f32[128,1,128]{2,1,0:T(1,128)}), f32[128,1,128]{2,1,0:T(1,128)S(1)}, u32[]{:S(2)}, u32[]{:S(2)}) %all-to-all-start) | async-done | bytes 65568 | tf_op jit(solution)/shard_map/all_to_all | solution.py:389
  23.3 1.3 %serve.1 = (f32[1024,128]{1,0:T(8,128)S(1)}, s32[8,128]{1,0:T(8,128)S(1)}, s32[256,128]{1,0:T(8,128)S(1)}, f32[1280,128]{1,0:T(8,128)S(1)}, f32[1280,128]{1,0:T(8,128)S(1)}, /*index=5*/f32[1280,128]{1,0:T(8,128)S(1)}) custom-call(s32[1]{0:T(128)} %bitcast.me_ref, f32[128,128]{1,0:T(8,128)S(1)} %bitcast.14, bf16[640,192]{1,0:T(8,128)(2,1)S(1)} %get-tuple-element.32.table_ref, ...), custom_call_target="tpu_custom_call" | custom-call | tf_op jit(solution)/shard_map/serve/pallas_call | solution.py:378
  24.6 18.1 %all_to_all.15 = f32[128,8,128]{2,1,0:T(8,128)S(1)} all-to-all(f32[128,8,128]{2,1,0:T(8,128)S(1)} %bitcast.13), channel_id=1, replica_groups=mesh['elem'=128] {'elem'}, dimensions={0} | all-to-all | bytes 1048576 | tf_op jit(solution)/shard_map/all_to_all | solution.py:389
  42.7 1.5 %finish.1 = (f32[1280,128]{1,0:T(8,128)S(1)}, f32[1024,128]{1,0:T(8,128)S(1)}) custom-call(s32[8,128]{1,0:T(8,128)S(1)} %get-tuple-element.35.ids_ref, f32[1024,128]{1,0:T(8,128)S(1)} %bitcast.11, s32[256,128]{1,0:T(8,128)S(1)} %get-tuple-element.37.level_ref, f32[1280,128]{1,0:T(8,128)S(1)} %get-tuple-element.38.c_ref, ...), custom_call_target="tpu_custom_call" | custom-call | tf_op jit(solution)/shard_map/finish/pallas_call | solution.py:378
  44.2 19.5 %all_to_all.16 = f32[128,1,1280]{2,1,0:T(1,128)S(1)} all-to-all(f32[128,1,1280]{2,1,0:T(1,128)S(1)} %bitcast.12), channel_id=1, replica_groups=mesh['elem'=128] {'elem'}, dimensions={0} | all-to-all | bytes 1310720 | tf_op jit(solution)/shard_map/all_to_all | solution.py:389
  63.8 1.9 %join.1 = f32[8,8,640]{2,1,0:T(8,128)} custom-call(s32[8,128]{1,0:T(8,128)S(1)} %get-tuple-element.26.peer_ref, f32[1280,128]{1,0:T(8,128)S(1)} %bitcast.10, bf16[1024,256]{1,0:T(8,128)(2,1)S(1)} %get-tuple-element.45.hot_ref, f32[1024,128]{1,0:T(8,128)S(1)} %get-tuple-element.46.home_ref), custom_call_target="tpu_custom_call" | custom-call | tf_op jit(solution)/shard_map/join/pallas_call | solution.py:446
Async XLA Ops:
  2.5 20.8 %all-to-all-start = ((f32[128,1,128]{2,1,0:T(1,128)}), f32[128,1,128]{2,1,0:T(1,128)S(1)}, u32[]{:S(2)}, u32[]{:S(2)}) async-start(f32[128,1,128]{2,1,0:T(1,128)} %bitcast.3), calls=%async_computation | async-start | bytes 131072 | tf_op jit(solution)/shard_map/all_to_all | solution.py:389

commit v3 on v2

--- a/solution.py
+++ b/solution.py
@@ -3,8 +3,11 @@
 from jax import lax
 from jax.experimental import pallas as pl
 from jax.experimental.pallas import tpu as pltpu
+from jax.sharding import Mesh
 from jax.sharding import PartitionSpec as P
 
+AXES = ("x", "y", "z", "core")
+GROUP = ("core", "z", "y", "x")
 GLL = (-1.0, -0.4472135954999579, 0.4472135954999579, 1.0)
 DEVS = 128
 ELEMS = 8
@@ -23,6 +26,11 @@
     return lax.broadcasted_iota(I32, shape, dim)
 
 
+def in_group(device):
+    core, z, y, x = device % 2, device // 2 % 4, device // 8 % 4, device // 32
+    return core * 64 + z * 16 + y * 4 + x
+
+
 def dot(a, b):
     return jnp.dot(a, b, preferred_element_type=F32)
 
@@ -43,7 +51,25 @@
     return high, mid, (rest - mid.astype(F32)).astype(BF16)
 
 
-def pack_kernel(me_ref, owner_hbm, local_hbm, coord_hbm, mass_hbm, old_hbm, tracer_hbm, req_ref, idx_ref, peer_ref, vals_ref, old_ref, tracer_ref, owner_ref, local_ref, coord_ref, mass_ref, sem):
+def ranks(owner):
+    sub = iota((DEVS, COLS), 0)
+    before = jnp.where(sub < iota((DEVS, COLS), 1), 1.0, 0.0).astype(BF16)
+    counter = jnp.concatenate([before, jnp.ones((COLS, COLS), BF16)], axis=1)
+    hots = [jnp.where(jnp.broadcast_to(owner[e : e + 1], (DEVS, COLS)) == sub, 1.0, 0.0) for e in range(ELEMS)]
+    counts = dot(jnp.concatenate(hots, axis=0).astype(BF16), counter)
+    parts = [counts[e * DEVS : (e + 1) * DEVS] for e in range(ELEMS)]
+    return hots, [p[:, :COLS] for p in parts], [p[:, COLS:] for p in parts]
+
+
+def spots(hots, inside, whole, base):
+    rows = []
+    for e in range(ELEMS):
+        rows.append(jnp.sum(hots[e] * (inside[e] + base), axis=0, keepdims=True))
+        base = base + whole[e]
+    return rows
+
+
+def pack_kernel(me_ref, owner_hbm, local_hbm, coord_hbm, mass_hbm, old_hbm, tracer_hbm, req_ref, away_ref, vals_ref, old_ref, tracer_ref, owner_ref, local_ref, coord_ref, mass_ref, sem):
     pairs = (
         (owner_hbm, owner_ref),
         (local_hbm, local_ref),
@@ -56,51 +82,28 @@
     for copy in copies:
         copy.start()
     me = me_ref[0]
-    sub = iota((DEVS, COLS), 0)
-    lane = iota((DEVS, COLS), 1)
-    before = jnp.where(sub < lane, 1.0, 0.0).astype(BF16)
-    counter = jnp.concatenate([before, jnp.ones((COLS, COLS), BF16)], axis=1)
-    earlier = jnp.where(lane < sub, 1.0, 0.0).astype(BF16)
     for copy in copies[:4]:
         copy.wait()
-    owner = owner_ref[...]
-    away = owner != me
-    owner = jnp.where(away, owner, -1)
+    owner = in_group(owner_ref[...])
+    owner = jnp.where(owner == me, -1, owner)
+    away_ref[...] = owner
     level = iota((ELEMS, COLS), 1) // NODES
     row = (local_ref[...] * LEVELS + (level + 1)).astype(F32)
     mass = mass_ref[...]
     vals_ref[:ELEMS] = row
     vals_ref[ELEMS : 2 * ELEMS] = coord_ref[0]
     vals_ref[2 * ELEMS : 3 * ELEMS] = coord_ref[1]
-    vals_ref[3 * ELEMS :] = jnp.where(away, 0.0, mass)
+    vals_ref[3 * ELEMS :] = jnp.where(owner < 0, mass, 0.0)
     values = (row, coord_ref[0], coord_ref[1], mass)
-    hots = [jnp.where(jnp.broadcast_to(owner[e : e + 1], (DEVS, COLS)) == sub, 1.0, 0.0) for e in range(ELEMS)]
-    counts = dot(jnp.concatenate(hots, axis=0).astype(BF16), counter)
-    total = counts[:DEVS, COLS:]
-    for e in range(1, ELEMS):
-        total = total + counts[e * DEVS : (e + 1) * DEVS, COLS:]
-    present = jnp.where(total > 0.0, 1.0, 0.0)
-    peer = dot(earlier, present.astype(BF16))
-    base = peer * float(SLOTS)
-    slot = sub % SLOTS
-    wide, places = [], []
-    for e in range(ELEMS):
-        part = counts[e * DEVS : (e + 1) * DEVS]
-        place = part[:, :COLS] + base
-        base = base + part[:, COLS:]
-        spot = jnp.sum(hots[e] * place, axis=0, keepdims=True).astype(I32)
-        places.append(spot)
+    hots, inside, whole = ranks(owner)
+    slot = (iota((DEVS, COLS), 0) % SLOTS).astype(F32)
+    wide = []
+    for e, spot in enumerate(spots(hots, inside, whole, jnp.zeros((DEVS, COLS), F32))):
         value = jnp.concatenate([jnp.broadcast_to(v[e : e + 1], (SLOTS, COLS)) for v in values], axis=0)
-        wide.append(jnp.where(jnp.broadcast_to(spot % SLOTS, (DEVS, COLS)) == slot, value, 0.0))
-    idx_ref[...] = jnp.where(away, jnp.concatenate(places, axis=0), -1).astype(F32)
+        wide.append(jnp.where(jnp.broadcast_to(spot, (DEVS, COLS)) == slot, value, 0.0))
     hot = jnp.concatenate(hots, axis=1).astype(BF16)
     high, mid = split2(jnp.concatenate(wide, axis=1))
     req_ref[...] = dot_nt(hot, high) + dot_nt(hot, mid)
-    owner_id = sub.astype(F32)
-    ids = [jnp.sum(jnp.where(peer == float(p), present, 0.0) * owner_id, axis=0, keepdims=True) for p in range(PEERS)]
-    named = jnp.sum(present, axis=0, keepdims=True)
-    ids = [ids[0]] + [jnp.where(named > float(p), ids[p], ids[0]) for p in range(1, PEERS)]
-    peer_ref[...] = jnp.concatenate(ids + [named] * (8 - PEERS), axis=0).astype(I32)
     for copy in copies[4:]:
         copy.wait()
 
@@ -187,7 +190,7 @@
     return clip, s_high + margin - clip, clip - s_low + margin
 
 
-def home_kernel(tracer_ref, old_ref, vals_ref, idx_ref, table_ref, bt_ref, part_ref, hot_ref, c_ref, up_ref, down_ref, scratch):
+def home_kernel(tracer_ref, old_ref, vals_ref, away_ref, table_ref, bt_ref, part_ref, hot_ref, peer_ref, c_ref, up_ref, down_ref, scratch):
     rows = ELEMS * LEVELS
     node = iota((NODES, COLS), 0)
     column = iota((NODES, COLS), 1)
@@ -227,7 +230,21 @@
     clip, up, down = level_sums(sums, hist, low, high)
     pad = jnp.zeros((Q, COLS - 3 * LEVELS), F32)
     part_ref[...] = jnp.concatenate([fold(source) - clip, up, down, pad], axis=1)
-    scratch[...] = jnp.concatenate([idx_ref[...], jnp.full((COLS - ELEMS, COLS), -1.0, F32)], axis=0).T
+    away = away_ref[...]
+    hots, inside, whole = ranks(away)
+    total = whole[0]
+    for e in range(1, ELEMS):
+        total = total + whole[e]
+    device = iota((DEVS, COLS), 0)
+    present = jnp.where(total > 0.0, 1.0, 0.0)
+    earlier = jnp.where(iota((DEVS, COLS), 1) < device, 1.0, 0.0).astype(BF16)
+    peer = dot(earlier, present.astype(BF16))
+    ids = [jnp.sum(jnp.where(peer == float(p), present, 0.0) * device.astype(F32), axis=0, keepdims=True) for p in range(PEERS)]
+    named = jnp.sum(present, axis=0, keepdims=True)
+    ids = [ids[0]] + [jnp.where(named > float(p), ids[p], ids[0]) for p in range(1, PEERS)]
+    peer_ref[...] = jnp.concatenate(ids + [named] * (8 - PEERS), axis=0).astype(I32)
+    place = jnp.where(away < 0, -1.0, jnp.concatenate(spots(hots, inside, whole, peer * float(SLOTS)), axis=0))
+    scratch[...] = jnp.concatenate([place, jnp.full((COLS - ELEMS, COLS), -1.0, F32)], axis=0).T
     turned = jnp.concatenate([scratch[pl.ds(k, LEVELS, stride=NODES), :] for k in range(NODES)], axis=0)
     lane = iota((COLS, SLOTS * 8), 1).astype(F32)
     for e in range(ELEMS):
@@ -235,7 +252,7 @@
         hot_ref[e * COLS : (e + 1) * COLS, :] = jnp.where(col == lane, 1.0, 0.0).astype(BF16)
 
 
-def serve_kernel(me_ref, req_ref, table_ref, part_ref, bt_ref, sums_ref, ids_ref, level_ref, c_ref, up_ref, down_ref, dense, tiles):
+def serve_kernel(me_ref, req_ref, table_ref, part_ref, bt_ref, keep_ref, give_ref, ids_ref, level_ref, c_ref, up_ref, down_ref, dense, tiles):
     req = req_ref[...]
     sub = iota((DEVS, DEVS), 0)
     lane = iota((DEVS, DEVS), 1)
@@ -275,53 +292,54 @@
         return carry[0] + s, carry[1] + h
 
     start = (jnp.zeros((2 * Q, 2 * LEVELS), F32), jnp.zeros((16, ELEMS * LEVELS), F32))
-    sums, hist = lax.fori_loop(0, (count + 7) // 8, step, start)
+    start = step(1, step(0, start))
+    sums, hist = lax.fori_loop(2, (count + 7) // 8, step, start)
     clip, up, down = level_sums(sums, hist, bt_ref[:Q, :], bt_ref[Q:, :])
     part = jnp.concatenate([-clip, up, down], axis=1) + part_ref[:, : 3 * LEVELS]
     packed = [part[8 * i : 8 * i + 8] for i in range(Q // 8)]
     packed.append(jnp.zeros((8, COLS - 3 * LEVELS * (Q // 8)), F32))
     packed = jnp.concatenate(packed, axis=1)
-    for d in range(DEVS):
-        sums_ref[8 * d : 8 * d + 8, :] = packed
-
-
-def finish_kernel(ids_ref, tot_ref, level_ref, c_ref, up_ref, down_ref, idx_ref, hc_ref, hu_ref, hd_ref, ans_ref, home_ref, rises, falls, scratch):
-    total = tot_ref[0:8, :]
-    for d in range(1, DEVS):
-        total = total + tot_ref[8 * d : 8 * d + 8, :]
+    upper = jnp.full((4, COLS), me_ref[0], I32) >= DEVS // 2
+    keep_ref[...] = jnp.where(upper, packed[4:], packed[:4])
+    give_ref[...] = jnp.where(upper, packed[:4], packed[4:])
+
+
+def spread_kernel(keep_ref, got_ref, sums_ref):
+    half = keep_ref[...] + got_ref[...]
+    both = jnp.concatenate([half, half], axis=0)
+    for d in range(DEVS // 2):
+        sums_ref[8 * d : 8 * d + 8, :] = both
+
+
+def finish_kernel(ids_ref, tot_ref, level_ref, c_ref, up_ref, down_ref, away_ref, hc_ref, hu_ref, hd_ref, ans_ref, home_ref, scratch):
+    halves = []
+    for core in range(2):
+        at = core * 4 * (DEVS // 2)
+        total = tot_ref[at : at + 8, :]
+        for d in range(1, DEVS // 4):
+            total = total + tot_ref[at + 8 * d : at + 8 * d + 8, :]
+        halves.append(total[:4] + total[4:])
+    total = jnp.concatenate(halves, axis=0)
     up_total = pltpu.roll(total, COLS - LEVELS, 1)
     down_total = pltpu.roll(total, COLS - 2 * LEVELS, 1)
-    rise = jnp.maximum(total, 0.0) / up_total
-    fall = jnp.minimum(total, 0.0) / down_total
-    home_level = iota((8, COLS), 1) // NODES
-    home_rise, home_fall = [], []
-    for i in range(Q // 8):
-        hr = hf = None
-        for l in range(LEVELS):
-            r = jnp.broadcast_to(rise[:, 24 * i + l : 24 * i + l + 1], (8, DEVS))
-            f = jnp.broadcast_to(fall[:, 24 * i + l : 24 * i + l + 1], (8, DEVS))
-            rises[i, l] = r
-            falls[i, l] = f
-            hr = r if hr is None else jnp.where(home_level == l, r, hr)
-            hf = f if hf is None else jnp.where(home_level == l, f, hf)
-        home_rise.append(hr)
-        home_fall.append(hf)
-    home_rise = jnp.concatenate(home_rise, axis=0)
-    home_fall = jnp.concatenate(home_fall, axis=0)
+    lanes = iota((8, COLS), 1)
+    real = (lanes < 3 * LEVELS * (Q // 8)) & (lanes % (3 * LEVELS) < LEVELS)
+    rise = jnp.where(real, jnp.maximum(total, 0.0) / up_total, 0.0)
+    fall = jnp.where(real, jnp.minimum(total, 0.0) / down_total, 0.0)
+    coef = [x[:, 24 * i : 24 * i + LEVELS] for x in (rise, fall) for i in range(Q // 8)]
+    coef = jnp.concatenate(split3(jnp.concatenate(coef, axis=0)), axis=1)
+
+    def by_level(level8):
+        hot = jnp.where(level8 == iota((8, 128), 0), 1.0, 0.0)
+        c = dot(coef, jnp.concatenate([hot] * 3, axis=0).astype(BF16))
+        return c[:Q], c[Q:]
+
     block = iota((CHUNK, DEVS), 1) // SLOTS
 
     def step(t, carry):
-        level8 = level_ref[pl.ds(pl.multiple_of(8 * t, 8), 8), :]
-        at_level = [level8 == l for l in range(LEVELS)]
-        out = []
-        for i in range(Q // 8):
-            r, f = rises[i, 0], falls[i, 0]
-            for l in range(1, LEVELS):
-                r = jnp.where(at_level[l], rises[i, l], r)
-                f = jnp.where(at_level[l], falls[i, l], f)
-            at = pl.ds(pl.multiple_of(Q * t + 8 * i, 8), 8)
-            out.append(c_ref[at, :] + r * up_ref[at, :] + f * down_ref[at, :])
-        out = jnp.concatenate(out, axis=0)
+        r, f = by_level(level_ref[pl.ds(pl.multiple_of(8 * t, 8), 8), :])
+        at = pl.ds(pl.multiple_of(Q * t, 8), Q)
+        out = c_ref[at, :] + r * up_ref[at, :] + f * down_ref[at, :]
         parts = [out[CHUNK * b : CHUNK * (b + 1)] for b in range(4)]
         for i in range(4):
             chunk = None
@@ -332,11 +350,14 @@
             ans_ref[pl.ds(ids_ref[0, 4 * t + i] * CHUNK, CHUNK), :] = chunk
         return carry
 
-    lax.fori_loop(0, (ids_ref[1, 0] + 3) // 4, step, 0)
+    for t in range(3):
+        step(t, 0)
+    lax.fori_loop(3, (ids_ref[1, 0] + 3) // 4, step, 0)
+    r, f = by_level(iota((8, COLS), 1) // NODES)
     for e in range(ELEMS):
         at = slice(e * Q, (e + 1) * Q)
-        v = hc_ref[at, :] + home_rise * hu_ref[at, :] + home_fall * hd_ref[at, :]
-        v = jnp.where(jnp.broadcast_to(idx_ref[e : e + 1, :], (Q, COLS)) < 0.0, v, 0.0)
+        v = hc_ref[at, :] + r * hu_ref[at, :] + f * hd_ref[at, :]
+        v = jnp.where(jnp.broadcast_to(away_ref[e : e + 1, :], (Q, COLS)) < 0, v, 0.0)
         scratch[e] = jnp.concatenate([v, jnp.zeros((COLS - Q, COLS), F32)], axis=0).T
         for k in range(NODES):
             home_ref[e * COLS + 8 * k : e * COLS + 8 * k + 8, :] = scratch[e, pl.ds(k, LEVELS, stride=NODES), :]
@@ -367,7 +388,7 @@
 
 
 def body(tracer, old_mass, new_mass, dep_owner, dep_local, dep_coord):
-    me = lax.axis_index("elem").astype(I32).reshape(1)
+    me = lax.axis_index(GROUP).astype(I32).reshape(1)
     owner = dep_owner.reshape(ELEMS, COLS)
     smem, vmem, hbm = (pl.BlockSpec(memory_space=m) for m in (pltpu.SMEM, pltpu.VMEM, pltpu.HBM))
 
@@ -386,16 +407,15 @@
         )(*args)
 
     def exchange(x, chunk):
-        y = lax.all_to_all(x.reshape((DEVS,) + chunk), "elem", 0, 0, tiled=True)
+        y = lax.all_to_all(x.reshape((DEVS,) + chunk), GROUP, 0, 0, tiled=True)
         return y.reshape(x.shape)
 
-    req, idx, peer, vals, old, table_in = call(
+    req, away, vals, old, near_tracer = call(
         pack_kernel,
         "pack",
         (
             ((DEVS, COLS), F32),
-            ((ELEMS, COLS), F32),
-            ((8, COLS), I32),
+            ((ELEMS, COLS), I32),
             ((4 * ELEMS, COLS), F32),
             ((ELEMS, COLS), F32),
             (tracer.shape, F32),
@@ -411,7 +431,7 @@
         [me] + [pltpu.with_memory_space_constraint(x, pltpu.HBM) for x in (owner, dep_local, dep_coord, new_mass, old_mass, tracer)],
     )
     asked = exchange(req, (1, COLS))
-    table, bt, part, hot, hc, hu, hd = call(
+    table, bt, part, hot, peer, hc, hu, hd = call(
         home_kernel,
         "home",
         (
@@ -419,28 +439,31 @@
             ((2 * Q, ELEMS * LEVELS), F32),
             ((Q, COLS), F32),
             ((ELEMS * COLS, SLOTS * 8), BF16),
+            ((8, COLS), I32),
         )
         + (((ELEMS * Q, COLS), F32),) * 3,
         [vmem] * 4,
         [pltpu.VMEM((COLS, COLS), F32)],
-        near(table_in, old, vals, idx),
-    )
-    sums, ids, level, c, up, down = call(
+        near(near_tracer, old, vals, away),
+    )
+    keep, give, ids, level, c, up, down = call(
         serve_kernel,
         "serve",
-        (((8 * DEVS, COLS), F32), ((8, DEVS), I32), ((2 * DEVS, DEVS), I32)) + (((SLOTS * Q, DEVS), F32),) * 3,
+        (((4, COLS), F32), ((4, COLS), F32), ((8, DEVS), I32), ((2 * DEVS, DEVS), I32)) + (((SLOTS * Q, DEVS), F32),) * 3,
         [smem] + [vmem] * 4,
         [pltpu.VMEM((DEVS, DEVS), F32), pltpu.VMEM((4, DEVS // 4, DEVS), F32)],
         [me] + near(asked, table, part, bt),
     )
-    totals = exchange(sums, (8, COLS))
+    given = lax.ppermute(give, "core", [(0, 1), (1, 0)])
+    (sums,) = call(spread_kernel, "spread", (((4 * DEVS, COLS), F32),), [vmem] * 2, [], near(keep, given))
+    totals = exchange(sums, (4, COLS))
     ans, home = call(
         finish_kernel,
         "finish",
         (((DEVS * CHUNK, 128), F32), ((ELEMS * COLS, 128), F32)),
         [smem] + [vmem] * 9,
-        [pltpu.VMEM((Q // 8, LEVELS, 8, DEVS), F32)] * 2 + [pltpu.VMEM((ELEMS, COLS, 128), F32)],
-        [ids] + near(totals, level, c, up, down, idx, hc, hu, hd),
+        [pltpu.VMEM((ELEMS, COLS, 128), F32)],
+        [ids] + near(totals, level, c, up, down, away, hc, hu, hd),
     )
     got = exchange(ans, (1, SLOTS * Q))
     return pl.pallas_call(
@@ -455,12 +478,13 @@
 
 
 def solution(mesh):
+    torus = Mesh(mesh.devices.reshape(4, 4, 4, 2), AXES)
     placed = (
-        P("elem", None, None),
-        P("elem", None),
-        P("elem", None),
-        P("elem", None, None),
-        P("elem", None),
-        P(None, "elem", None),
-    )
-    return jax.shard_map(body, mesh=mesh, in_specs=placed, out_specs=P("elem", None, None), check_vma=False)
+        P(AXES, None, None),
+        P(AXES, None),
+        P(AXES, None),
+        P(AXES, None, None),
+        P(AXES, None),
+        P(None, AXES, None),
+    )
+    return jax.shard_map(body, mesh=torus, in_specs=placed, out_specs=P(AXES, None, None), check_vma=False)

time: 65.8 us -> 62.6 us (0.951)
  blocking collectives: 37.6 us -> 33 us
  waiting for transfers between devices: 7.55 us -> 8.45 us
  starting transfers between devices: 11.5 us -> 12.3 us
    all_to_all x2, blocking collectives: 37.6 us -> 33 us  [exchange(): y = lax.all_to_all(x.reshape((DEVS,) + chunk), GROUP, 0, 0, tiled=True)]
    ppermute x0 -> x1, waiting for transfers between devices: none -> 0.82 us  [body(): given = lax.ppermute(give, 'core', [(0, 1), (1, 0)])]
    ppermute x0 -> x1, starting transfers between devices: none -> 0.76 us  [body(): given = lax.ppermute(give, 'core', [(0, 1), (1, 0)])]
    pallas_call x4 -> x5, Pallas kernels: 7.05 us -> 6.9 us  [call(): pl.pallas_call(kernel, out_shape=tuple((pltpu.VMEM(shape, dtype) for shap...]
  transfers between devices with their start and end apart: 1 -> 2, of which waited for: 1 -> 2; matrix products, arithmetic and copies ran while one was open for 0% -> 0% of each run, Pallas kernels for 3% -> 3%
where the time goes in v3:
time: 62.6 us; the launch traced here: 62.5 us
  blocking collectives  33 us (53%)
  starting transfers between devices  12.3 us (20%)
  Pallas kernels  8.76 us (14%)
  waiting for transfers between devices  8.45 us (13%)
    all_to_all x2, blocking collectives, exchange(): y = lax.all_to_all(x.reshape((DEVS,) + chunk), GROUP, 0, 0, tiled=True)  33 us
    all_to_all x1, starting transfers between devices, exchange(): y = lax.all_to_all(x.reshape((DEVS,) + chunk), GROUP, 0, 0, tiled=True)  11.5 us
    all_to_all x1, waiting for transfers between devices, exchange(): y = lax.all_to_all(x.reshape((DEVS,) + chunk), GROUP, 0, 0, tiled=True)  7.63 us
    pallas_call x5, Pallas kernels, call(): pl.pallas_call(kernel, out_shape=tuple((pltpu.VMEM(shape, dtype) for shap...  6.9 us
    pallas_call x1, Pallas kernels, body(): pl.pallas_call(join_kernel, out_shape=jax.ShapeDtypeStruct((ELEMS, LEVELS...  1.86 us
  transfers between devices with their start and end apart: 2, of which 2 were waited for; matrix products, arithmetic and copies ran while one was open for 0% of the time, Pallas kernels for 3%

profile of v3, /device:TPU:1, one launch (start us, length us, event | category | flops | bytes accessed | tf_op | source)
XLA Modules:
  0.0 62.5 jit_solution(4572880874649743412)
XLA Ops:
  0.0 2.2 %pack.1 = (f32[128,128]{1,0:T(8,128)}, s32[8,128]{1,0:T(8,128)S(1)}, f32[32,128]{1,0:T(8,128)S(1)}, f32[8,128]{1,0:T(8,128)S(1)}, f32[8,8,640]{2,1,0:T(8,128)S(1)}) custom-call(s32[1]{0:T(128)} %bitcast.me_ref, s32[8,128]{1,0:T(8,128)} %bitcast.15, s32[8,128]{1,0:T(8,128)} %local_hbm.1, f32[2,8,128]{2,1,0:T(8,128)} %coord_hbm.1, f32[8,128]{1,0:T(8,128)} %mass_hbm.1, ...), custom_call_target="tpu_custom_call" | custom-call | tf_op jit(solution)/shard_map/pack/pallas_call | solution.py:399
  2.2 11.5 %all-to-all-start = ((f32[128,1,128]{2,1,0:T(1,128)}), f32[128,1,128]{2,1,0:T(1,128)S(1)}, u32[]{:S(2)}, u32[]{:S(2)}) async-start(f32[128,1,128]{2,1,0:T(1,128)} %bitcast.3), calls=%async_computation | async-start | bytes 131072 | tf_op jit(solution)/shard_map/all_to_all | solution.py:410
  13.7 1.8 %home.1 = (bf16[640,192]{1,0:T(8,128)(2,1)S(1)}, f32[80,64]{1,0:T(8,128)S(1)}, f32[40,128]{1,0:T(8,128)S(1)}, bf16[1024,256]{1,0:T(8,128)(2,1)S(1)}, s32[8,128]{...) custom-call(f32[8,8,640]{2,1,0:T(8,128)S(1)} %get-tuple-element.27.tracer_ref, ...), custom_call_target="tpu_custom_call" | custom-call | tf_op jit(solution)/shard_map/home/pallas_call | solution.py:399
  15.5 7.6 %all-to-all-done = f32[128,1,128]{2,1,0:T(1,128)S(1)} async-done(((f32[128,1,128]{2,1,0:T(1,128)}), f32[128,1,128]{2,1,0:T(1,128)S(1)}, u32[]{:S(2)}, u32[]{:S(2)}) %all-to-all-start) | async-done | bytes 65568 | tf_op jit(solution)/shard_map/all_to_all | solution.py:410
  23.2 1.3 %serve.1 = (f32[4,128]{1,0:T(4,128)S(1)}, f32[4,128]{1,0:T(4,128)S(1)}, s32[8,128]{1,0:T(8,128)S(1)}, s32[256,128]{1,0:T(8,128)S(1)}, f32[1280,128]{1,0:T(8,128)...) custom-call(s32[1]{0:T(128)} %bitcast.me_ref, f32[128,128]{1,0:T(8,128)S(1)} %bitcast.14, ...), custom_call_target="tpu_custom_call" | custom-call | tf_op jit(solution)/shard_map/serve/pallas_call | solution.py:399
  24.5 0.8 %collective-permute-start = (f32[4,128]{1,0:T(4,128)S(1)}, f32[4,128]{1,0:T(4,128)S(1)}, u32[]{:S(2)}, u32[]{:S(2)}) collective-permute-start(f32[4,128]{1,0:T(4,128)S(1)} %get-tuple-element.38), channel_id=1, source_target_pairs={{0,1},{1,0},{2,3},{3,2},{4,5},{5,4},{6,7},{7,6},{8,9},{9,8},{10,11... | collective-permute-start | bytes 6152 | tf_op jit(solution)/shard_map/ppermute | solution.py:457
  25.2 0.8 %collective-permute-done.got_ref = f32[4,128]{1,0:T(4,128)S(1)} collective-permute-done((f32[4,128]{1,0:T(4,128)S(1)}, f32[4,128]{1,0:T(4,128)S(1)}, u32[]{:S(2)}, u32[]{:S(2)}) %collective-permute-start) | collective-permute-done | bytes 2080 | tf_op jit(solution)/shard_map/ppermute | solution.py:457
  26.1 14.3 %all_to_all.15 = f32[128,4,128]{2,1,0:T(4,128)S(1)} all-to-all(f32[128,4,128]{2,1,0:T(4,128)S(1)} %bitcast.11), channel_id=1, replica_groups=mesh['x'=4,'y'=4,'z'=4,'core'=2] {'core','z','y','x'}, dimensions={0} | all-to-all | bytes 524288 | tf_op jit(solution)/shard_map/all_to_all | solution.py:410
  40.4 1.5 %finish.1 = (f32[1280,128]{1,0:T(8,128)S(1)}, f32[1024,128]{1,0:T(8,128)S(1)}) custom-call(s32[8,128]{1,0:T(8,128)S(1)} %get-tuple-element.36.ids_ref, f32[512,128]{1,0:T(8,128)S(1)} %bitcast.12, s32[256,128]{1,0:T(8,128)S(1)} %get-tuple-element.39.level_ref, f32[1280,128]{1,0:T(8,128)S(1)} %get-tuple-element.40.c_ref, ...), custom_call_target="tpu_custom_call" | custom-call | tf_op jit(solution)/shard_map/finish/pallas_call | solution.py:399
  41.9 18.7 %all_to_all.16 = f32[128,1,1280]{2,1,0:T(1,128)S(1)} all-to-all(f32[128,1,1280]{2,1,0:T(1,128)S(1)} %bitcast.13), channel_id=1, replica_groups=mesh['x'=4,'y'=4,'z'=4,'core'=2] {'core','z','y','x'}, dimensions={0} | all-to-all | bytes 1310720 | tf_op jit(solution)/shard_map/all_to_all | solution.py:410
  60.6 1.9 %join.1 = f32[8,8,640]{2,1,0:T(8,128)} custom-call(s32[8,128]{1,0:T(8,128)S(1)} %get-tuple-element.31.peer_ref, f32[1280,128]{1,0:T(8,128)S(1)} %bitcast.10, bf16[1024,256]{1,0:T(8,128)(2,1)S(1)} %get-tuple-element.47.hot_ref, f32[1024,128]{1,0:T(8,128)S(1)} %get-tuple-element.48.home_ref), custom_call_target="tpu_custom_call" | custom-call | tf_op jit(solution)/shard_map/join/pallas_call | solution.py:469
  (1 shorter events, 0.0 us)
Async XLA Ops:
  2.2 21.0 %all-to-all-start = ((f32[128,1,128]{2,1,0:T(1,128)}), f32[128,1,128]{2,1,0:T(1,128)S(1)}, u32[]{:S(2)}, u32[]{:S(2)}) async-start(f32[128,1,128]{2,1,0:T(1,128)} %bitcast.3), calls=%async_computation | async-start | bytes 131072 | tf_op jit(solution)/shard_map/all_to_all | solution.py:410
  24.5 1.6 %collective-permute-start = (f32[4,128]{1,0:T(4,128)S(1)}, f32[4,128]{1,0:T(4,128)S(1)}, u32[]{:S(2)}, u32[]{:S(2)}) collective-permute-start(f32[4,128]{1,0:T(4,128)S(1)} %get-tuple-element.38), channel_id=1, source_target_pairs={{0,1},{1,0},{2,3},{3,2},{4,5},{5,4},{6,7},{7,6},{8,9},{9,8},{10,11... | collective-permute-start | bytes 6152 | tf_op jit(solution)/shard_map/ppermute | solution.py:457

commit v4 on v3

--- a/solution.py
+++ b/solution.py
@@ -311,7 +311,7 @@
         sums_ref[8 * d : 8 * d + 8, :] = both
 
 
-def finish_kernel(ids_ref, tot_ref, level_ref, c_ref, up_ref, down_ref, away_ref, hc_ref, hu_ref, hd_ref, ans_ref, home_ref, scratch):
+def finish_kernel(ids_ref, tot_ref, level_ref, c_ref, up_ref, down_ref, away_ref, hc_ref, hu_ref, hd_ref, ans_ref, home_ref, scratch, later, sem):
     halves = []
     for core in range(2):
         at = core * 4 * (DEVS // 2)
@@ -336,7 +336,9 @@
 
     block = iota((CHUNK, DEVS), 1) // SLOTS
 
-    def step(t, carry):
+    first = ids_ref[...]
+
+    def step(t, id_of):
         r, f = by_level(level_ref[pl.ds(pl.multiple_of(8 * t, 8), 8), :])
         at = pl.ds(pl.multiple_of(Q * t, 8), Q)
         out = c_ref[at, :] + r * up_ref[at, :] + f * down_ref[at, :]
@@ -347,12 +349,24 @@
                 shift = (b - i) * SLOTS % DEVS
                 moved = pltpu.roll(parts[b], shift, 1) if shift else parts[b]
                 chunk = moved if chunk is None else jnp.where(block == b, moved, chunk)
-            ans_ref[pl.ds(ids_ref[0, 4 * t + i] * CHUNK, CHUNK), :] = chunk
-        return carry
+            ans_ref[pl.ds(id_of(4 * t + i) * CHUNK, CHUNK), :] = chunk
 
     for t in range(3):
-        step(t, 0)
-    lax.fori_loop(3, (ids_ref[1, 0] + 3) // 4, step, 0)
+        step(t, lambda i: first[0, i])
+    count = first[1, 0]
+
+    @pl.when(count > 12)
+    def _():
+        copy = pltpu.make_async_copy(ids_ref, later, sem)
+        copy.start()
+        copy.wait()
+
+        def more(t, carry):
+            step(t, lambda i: later[0, i])
+            return carry
+
+        lax.fori_loop(3, (count + 3) // 4, more, 0)
+
     r, f = by_level(iota((8, COLS), 1) // NODES)
     for e in range(ELEMS):
         at = slice(e * Q, (e + 1) * Q)
@@ -365,7 +379,8 @@
 
 def join_kernel(peer_ref, ans_ref, hot_ref, home_ref, out_hbm, out_ref, sem):
     block = iota((CHUNK, 128), 1) // SLOTS
-    chunks = [ans_ref[pl.ds(peer_ref[p, 0] * CHUNK, CHUNK), :] for p in range(PEERS)]
+    peers = peer_ref[...]
+    chunks = [ans_ref[pl.ds(peers[p, 0] * CHUNK, CHUNK), :] for p in range(PEERS)]
     table = []
     for b in range(4):
 
@@ -461,20 +476,20 @@
         finish_kernel,
         "finish",
         (((DEVS * CHUNK, 128), F32), ((ELEMS * COLS, 128), F32)),
-        [smem] + [vmem] * 9,
-        [pltpu.VMEM((ELEMS, COLS, 128), F32)],
-        [ids] + near(totals, level, c, up, down, away, hc, hu, hd),
+        [vmem] * 10,
+        [pltpu.VMEM((ELEMS, COLS, 128), F32), pltpu.SMEM((8, DEVS), I32), pltpu.SemaphoreType.DMA],
+        near(ids, totals, level, c, up, down, away, hc, hu, hd),
     )
     got = exchange(ans, (1, SLOTS * Q))
     return pl.pallas_call(
         join_kernel,
         out_shape=jax.ShapeDtypeStruct((ELEMS, LEVELS, NODES * Q), F32),
-        in_specs=[smem] + [vmem] * 3,
+        in_specs=[vmem] * 4,
         out_specs=hbm,
         scratch_shapes=[pltpu.VMEM((ELEMS, LEVELS, NODES * Q), F32), pltpu.SemaphoreType.DMA((ELEMS,))],
         compiler_params=pltpu.CompilerParams(vmem_limit_bytes=20 << 20),
         name="join",
-    )(peer, *near(got, hot, home))
+    )(*near(peer, got, hot, home))
 
 
 def solution(mesh):

time: 62.6 us -> 61.5 us (0.982)
  Pallas kernels: 8.76 us -> 7.6 us
where the time goes in v4:
time: 61.5 us; the launch traced here: 61.3 us
  blocking collectives  33 us (54%)
  starting transfers between devices  12.3 us (20%)
  waiting for transfers between devices  8.45 us (14%)
  Pallas kernels  7.6 us (12%)
    all_to_all x2, blocking collectives, exchange(): y = lax.all_to_all(x.reshape((DEVS,) + chunk), GROUP, 0, 0, tiled=True)  33 us
    all_to_all x1, starting transfers between devices, exchange(): y = lax.all_to_all(x.reshape((DEVS,) + chunk), GROUP, 0, 0, tiled=True)  11.5 us
    all_to_all x1, waiting for transfers between devices, exchange(): y = lax.all_to_all(x.reshape((DEVS,) + chunk), GROUP, 0, 0, tiled=True)  7.63 us
    pallas_call x5, Pallas kernels, call(): pl.pallas_call(kernel, out_shape=tuple((pltpu.VMEM(shape, dtype) for shap...  6.31 us
    pallas_call x1, Pallas kernels, body(): pl.pallas_call(join_kernel, out_shape=jax.ShapeDtypeStruct((ELEMS, LEVELS...  1.29 us
  transfers between devices with their start and end apart: 2, of which 2 were waited for; matrix products, arithmetic and copies ran while one was open for 0% of the time, Pallas kernels for 3%

profile of v4, /device:TPU:1, one launch (start us, length us, event | category | flops | bytes accessed | tf_op | source)
XLA Modules:
  0.0 61.3 jit_solution(7850048776380550669)
XLA Ops:
  0.0 2.2 %pack.1 = (f32[128,128]{1,0:T(8,128)}, s32[8,128]{1,0:T(8,128)S(1)}, f32[32,128]{1,0:T(8,128)S(1)}, f32[8,128]{1,0:T(8,128)S(1)}, f32[8,8,640]{2,1,0:T(8,128)S(1)}) custom-call(s32[1]{0:T(128)} %bitcast.me_ref, s32[8,128]{1,0:T(8,128)} %bitcast.15, s32[8,128]{1,0:T(8,128)} %local_hbm.1, f32[2,8,128]{2,1,0:T(8,128)} %coord_hbm.1, f32[8,128]{1,0:T(8,128)} %mass_hbm.1, ...), custom_call_target="tpu_custom_call" | custom-call | tf_op jit(solution)/shard_map/pack/pallas_call | solution.py:414
  2.2 11.5 %all-to-all-start = ((f32[128,1,128]{2,1,0:T(1,128)}), f32[128,1,128]{2,1,0:T(1,128)S(1)}, u32[]{:S(2)}, u32[]{:S(2)}) async-start(f32[128,1,128]{2,1,0:T(1,128)} %bitcast.3), calls=%async_computation | async-start | bytes 131072 | tf_op jit(solution)/shard_map/all_to_all | solution.py:425
  13.7 1.8 %home.1 = (bf16[640,192]{1,0:T(8,128)(2,1)S(1)}, f32[80,64]{1,0:T(8,128)S(1)}, f32[40,128]{1,0:T(8,128)S(1)}, bf16[1024,256]{1,0:T(8,128)(2,1)S(1)}, s32[8,128]{...) custom-call(f32[8,8,640]{2,1,0:T(8,128)S(1)} %get-tuple-element.27.tracer_ref, ...), custom_call_target="tpu_custom_call" | custom-call | tf_op jit(solution)/shard_map/home/pallas_call | solution.py:414
  15.5 7.6 %all-to-all-done = f32[128,1,128]{2,1,0:T(1,128)S(1)} async-done(((f32[128,1,128]{2,1,0:T(1,128)}), f32[128,1,128]{2,1,0:T(1,128)S(1)}, u32[]{:S(2)}, u32[]{:S(2)}) %all-to-all-start) | async-done | bytes 65568 | tf_op jit(solution)/shard_map/all_to_all | solution.py:425
  23.2 1.3 %serve.1 = (f32[4,128]{1,0:T(4,128)S(1)}, f32[4,128]{1,0:T(4,128)S(1)}, s32[8,128]{1,0:T(8,128)S(1)}, s32[256,128]{1,0:T(8,128)S(1)}, f32[1280,128]{1,0:T(8,128)...) custom-call(s32[1]{0:T(128)} %bitcast.me_ref, f32[128,128]{1,0:T(8,128)S(1)} %bitcast.14, ...), custom_call_target="tpu_custom_call" | custom-call | tf_op jit(solution)/shard_map/serve/pallas_call | solution.py:414
  24.5 0.8 %collective-permute-start = (f32[4,128]{1,0:T(4,128)S(1)}, f32[4,128]{1,0:T(4,128)S(1)}, u32[]{:S(2)}, u32[]{:S(2)}) collective-permute-start(f32[4,128]{1,0:T(4,128)S(1)} %get-tuple-element.38), channel_id=1, source_target_pairs={{0,1},{1,0},{2,3},{3,2},{4,5},{5,4},{6,7},{7,6},{8,9},{9,8},{10,11... | collective-permute-start | bytes 6152 | tf_op jit(solution)/shard_map/ppermute | solution.py:472
  25.2 0.8 %collective-permute-done.got_ref = f32[4,128]{1,0:T(4,128)S(1)} collective-permute-done((f32[4,128]{1,0:T(4,128)S(1)}, f32[4,128]{1,0:T(4,128)S(1)}, u32[]{:S(2)}, u32[]{:S(2)}) %collective-permute-start) | collective-permute-done | bytes 2080 | tf_op jit(solution)/shard_map/ppermute | solution.py:472
  26.1 14.3 %all_to_all.15 = f32[128,4,128]{2,1,0:T(4,128)S(1)} all-to-all(f32[128,4,128]{2,1,0:T(4,128)S(1)} %bitcast.11), channel_id=1, replica_groups=mesh['x'=4,'y'=4,'z'=4,'core'=2] {'core','z','y','x'}, dimensions={0} | all-to-all | bytes 524288 | tf_op jit(solution)/shard_map/all_to_all | solution.py:425
  40.4 0.9 %finish.1 = (f32[1280,128]{1,0:T(8,128)S(1)}, f32[1024,128]{1,0:T(8,128)S(1)}) custom-call(s32[8,128]{1,0:T(8,128)S(1)} %get-tuple-element.36.ids_ref, f32[512,128]{1,0:T(8,128)S(1)} %bitcast.12, s32[256,128]{1,0:T(8,128)S(1)} %get-tuple-element.39.level_ref, f32[1280,128]{1,0:T(8,128)S(1)} %get-tuple-element.40.c_ref, ...), custom_call_target="tpu_custom_call" | custom-call | tf_op jit(solution)/shard_map/finish/pallas_call | solution.py:414
  41.4 18.6 %all_to_all.16 = f32[128,1,1280]{2,1,0:T(1,128)S(1)} all-to-all(f32[128,1,1280]{2,1,0:T(1,128)S(1)} %bitcast.13), channel_id=1, replica_groups=mesh['x'=4,'y'=4,'z'=4,'core'=2] {'core','z','y','x'}, dimensions={0} | all-to-all | bytes 1310720 | tf_op jit(solution)/shard_map/all_to_all | solution.py:425
  60.0 1.3 %join.1 = f32[8,8,640]{2,1,0:T(8,128)} custom-call(s32[8,128]{1,0:T(8,128)S(1)} %get-tuple-element.31.peer_ref, f32[1280,128]{1,0:T(8,128)S(1)} %bitcast.10, bf16[1024,256]{1,0:T(8,128)(2,1)S(1)} %get-tuple-element.47.hot_ref, f32[1024,128]{1,0:T(8,128)S(1)} %get-tuple-element.48.home_ref), custom_call_target="tpu_custom_call" | custom-call | tf_op jit(solution)/shard_map/join/pallas_call | solution.py:484
  (1 shorter events, 0.0 us)
Async XLA Ops:
  2.2 21.0 %all-to-all-start = ((f32[128,1,128]{2,1,0:T(1,128)}), f32[128,1,128]{2,1,0:T(1,128)S(1)}, u32[]{:S(2)}, u32[]{:S(2)}) async-start(f32[128,1,128]{2,1,0:T(1,128)} %bitcast.3), calls=%async_computation | async-start | bytes 131072 | tf_op jit(solution)/shard_map/all_to_all | solution.py:425
  24.5 1.6 %collective-permute-start = (f32[4,128]{1,0:T(4,128)S(1)}, f32[4,128]{1,0:T(4,128)S(1)}, u32[]{:S(2)}, u32[]{:S(2)}) collective-permute-start(f32[4,128]{1,0:T(4,128)S(1)} %get-tuple-element.38), channel_id=1, source_target_pairs={{0,1},{1,0},{2,3},{3,2},{4,5},{5,4},{6,7},{7,6},{8,9},{9,8},{10,11... | collective-permute-start | bytes 6152 | tf_op jit(solution)/shard_map/ppermute | solution.py:472

commit v5 on v4

--- a/solution.py
+++ b/solution.py
@@ -190,7 +190,7 @@
     return clip, s_high + margin - clip, clip - s_low + margin
 
 
-def home_kernel(tracer_ref, old_ref, vals_ref, away_ref, table_ref, bt_ref, part_ref, hot_ref, peer_ref, c_ref, up_ref, down_ref, scratch):
+def home_kernel(tracer_ref, old_ref, vals_ref, away_ref, table_ref, bt_ref, part_ref, hot_ref, peer_ref, c_ref, up_ref, down_ref, scratch, turns):
     rows = ELEMS * LEVELS
     node = iota((NODES, COLS), 0)
     column = iota((NODES, COLS), 1)
@@ -220,13 +220,17 @@
         clipped, highest, lowest, s, h, _ = evaluate(*args, table, consts)
         sums = s if sums is None else sums + s
         hist = h if hist is None else hist + h
-        for i in range(Q // 8):
-            up, down = spread_terms(clipped[i], highest[i], lowest[i])
-            for j in range(2):
-                at = slice((e + j) * Q + 8 * i, (e + j) * Q + 8 * i + 8)
-                c_ref[at, :] = clipped[i][:, j * COLS : (j + 1) * COLS]
-                up_ref[at, :] = up[:, j * COLS : (j + 1) * COLS]
-                down_ref[at, :] = down[:, j * COLS : (j + 1) * COLS]
+        terms = [spread_terms(clipped[i], highest[i], lowest[i]) for i in range(Q // 8)]
+        terms = (clipped, [t[0] for t in terms], [t[1] for t in terms])
+        for j in range(2):
+            stays = jnp.broadcast_to(away_ref[e + j : e + j + 1, :], (Q, COLS)) < 0
+            for x, (term, ref) in enumerate(zip(terms, (c_ref, up_ref, down_ref))):
+                v = jnp.concatenate([t[:, j * COLS : (j + 1) * COLS] for t in term], axis=0)
+                v = jnp.concatenate([jnp.where(stays, v, 0.0), jnp.zeros((COLS - Q, COLS), F32)], axis=0)
+                turns[x, e + j] = v.T
+                for k in range(NODES):
+                    at = (e + j) * COLS + LEVELS * k
+                    ref[at : at + LEVELS, :] = turns[x, e + j, pl.ds(k, LEVELS, stride=NODES), :]
     clip, up, down = level_sums(sums, hist, low, high)
     pad = jnp.zeros((Q, COLS - 3 * LEVELS), F32)
     part_ref[...] = jnp.concatenate([fold(source) - clip, up, down, pad], axis=1)
@@ -259,13 +263,16 @@
     high, mid = split2(req)
     first = jnp.where(iota((16, DEVS), 1) == 0, 1.0, 0.0).astype(BF16)
     asks = jnp.where(dot_nt(first, high) > 0.0, 1.0, 0.0)
-    place = dot(asks.astype(BF16), jnp.where(sub < lane, 1.0, 0.0).astype(BF16))
-    count = jnp.sum(asks[0:1]).astype(I32)
+    counter = jnp.concatenate([jnp.where(sub < lane, 1.0, 0.0).astype(BF16), jnp.ones((DEVS, DEVS), BF16)], axis=1)
+    place = dot(asks.astype(BF16), counter)
+    counted = place[:8, DEVS:].astype(I32)
+    place = place[:, :DEVS]
+    count = counted[0, 0]
     pick = jnp.where(jnp.broadcast_to(place[0:1], (DEVS, DEVS)) == sub.astype(F32), jnp.broadcast_to(asks[0:1], (DEVS, DEVS)), 0.0).astype(BF16)
-    dense[...] = dot(pick, high) + dot(pick, mid)
+    dense[...] = dot(jnp.concatenate([pick, pick], axis=1), jnp.concatenate([high, mid], axis=0))
     ids = dot_nt(iota((16, DEVS), 1).astype(F32).astype(BF16), pick)[:8].astype(I32)
-    ids = jnp.where(iota((8, DEVS), 1) < count, ids, me_ref[0])
-    ids_ref[...] = jnp.where(iota((8, DEVS), 0) == 0, ids, count)
+    ids = jnp.where(iota((8, DEVS), 1) < counted, ids, me_ref[0])
+    ids_ref[...] = jnp.where(iota((8, DEVS), 0) == 0, ids, counted)
     groups = [dense[pl.ds(i, DEVS // 4, stride=4), :] for i in range(4)]
     block = iota((DEVS // 4, DEVS), 1) // SLOTS
     for v in range(4):
@@ -311,7 +318,7 @@
         sums_ref[8 * d : 8 * d + 8, :] = both
 
 
-def finish_kernel(ids_ref, tot_ref, level_ref, c_ref, up_ref, down_ref, away_ref, hc_ref, hu_ref, hd_ref, ans_ref, home_ref, scratch, later, sem):
+def finish_kernel(ids_ref, tot_ref, level_ref, c_ref, up_ref, down_ref, hc_ref, hu_ref, hd_ref, ans_ref, home_ref, later, sem):
     halves = []
     for core in range(2):
         at = core * 4 * (DEVS // 2)
@@ -327,7 +334,10 @@
     rise = jnp.where(real, jnp.maximum(total, 0.0) / up_total, 0.0)
     fall = jnp.where(real, jnp.minimum(total, 0.0) / down_total, 0.0)
     coef = [x[:, 24 * i : 24 * i + LEVELS] for x in (rise, fall) for i in range(Q // 8)]
-    coef = jnp.concatenate(split3(jnp.concatenate(coef, axis=0)), axis=1)
+    coef = jnp.concatenate(coef, axis=0)
+    square = jnp.concatenate([coef, jnp.zeros((2 * Q, 128 - LEVELS), F32)], axis=1)
+    turned = jnp.concatenate([square, jnp.zeros((128 - 2 * Q, 128), F32)], axis=0).T[:LEVELS]
+    coef = jnp.concatenate(split3(coef), axis=1)
 
     def by_level(level8):
         hot = jnp.where(level8 == iota((8, 128), 0), 1.0, 0.0)
@@ -366,15 +376,11 @@
             return carry
 
         lax.fori_loop(3, (count + 3) // 4, more, 0)
-
-    r, f = by_level(iota((8, COLS), 1) // NODES)
+    rises = jnp.concatenate([turned] * NODES, axis=0)
+    falls = jnp.concatenate([pltpu.roll(turned, 128 - Q, 1)] * NODES, axis=0)
     for e in range(ELEMS):
-        at = slice(e * Q, (e + 1) * Q)
-        v = hc_ref[at, :] + r * hu_ref[at, :] + f * hd_ref[at, :]
-        v = jnp.where(jnp.broadcast_to(away_ref[e : e + 1, :], (Q, COLS)) < 0, v, 0.0)
-        scratch[e] = jnp.concatenate([v, jnp.zeros((COLS - Q, COLS), F32)], axis=0).T
-        for k in range(NODES):
-            home_ref[e * COLS + 8 * k : e * COLS + 8 * k + 8, :] = scratch[e, pl.ds(k, LEVELS, stride=NODES), :]
+        at = slice(e * COLS, (e + 1) * COLS)
+        home_ref[at, :] = hc_ref[at, :] + rises * hu_ref[at, :] + falls * hd_ref[at, :]
 
 
 def join_kernel(peer_ref, ans_ref, hot_ref, home_ref, out_hbm, out_ref, sem):
@@ -395,7 +401,8 @@
     high, mid = split2(jnp.concatenate(table, axis=0))
     for e in range(ELEMS):
         hot = hot_ref[e * COLS : (e + 1) * COLS, :]
-        v = dot_nt(hot, high) + dot_nt(hot, mid) + home_ref[e * COLS : (e + 1) * COLS, :Q]
+        at = slice(e * COLS, (e + 1) * COLS)
+        v = dot_nt(hot, high) + dot_nt(hot, mid) + home_ref[at, :Q]
         out_ref[e] = jnp.concatenate([v[8 * k : 8 * k + 8] for k in range(NODES)], axis=1)
         pltpu.make_async_copy(out_ref.at[e], out_hbm.at[e], sem.at[e]).start()
     for e in range(ELEMS):
@@ -456,9 +463,9 @@
             ((ELEMS * COLS, SLOTS * 8), BF16),
             ((8, COLS), I32),
         )
-        + (((ELEMS * Q, COLS), F32),) * 3,
+        + (((ELEMS * COLS, 128), F32),) * 3,
         [vmem] * 4,
-        [pltpu.VMEM((COLS, COLS), F32)],
+        [pltpu.VMEM((COLS, COLS), F32), pltpu.VMEM((3, ELEMS, COLS, 128), F32)],
         near(near_tracer, old, vals, away),
     )
     keep, give, ids, level, c, up, down = call(
@@ -476,9 +483,9 @@
         finish_kernel,
         "finish",
         (((DEVS * CHUNK, 128), F32), ((ELEMS * COLS, 128), F32)),
-        [vmem] * 10,
-        [pltpu.VMEM((ELEMS, COLS, 128), F32), pltpu.SMEM((8, DEVS), I32), pltpu.SemaphoreType.DMA],
-        near(ids, totals, level, c, up, down, away, hc, hu, hd),
+        [vmem] * 9,
+        [pltpu.SMEM((8, DEVS), I32), pltpu.SemaphoreType.DMA],
+        near(ids, totals, level, c, up, down, hc, hu, hd),
     )
     got = exchange(ans, (1, SLOTS * Q))
     return pl.pallas_call(

time: 61.5 us -> 61.2 us (level)
  transfers between devices with their start and end apart: 2 -> 2, of which waited for: 2 -> 2; matrix products, arithmetic and copies ran while one was open for 0% -> 0% of each run, Pallas kernels for 3% -> 4%
where the time goes in v5:
time: 61.2 us; the launch traced here: 61 us
  blocking collectives  33 us (54%)
  starting transfers between devices  12.2 us (20%)
  waiting for transfers between devices  8.03 us (13%)
  Pallas kernels  7.75 us (13%)
    all_to_all x2, blocking collectives, exchange(): y = lax.all_to_all(x.reshape((DEVS,) + chunk), GROUP, 0, 0, tiled=True)  33 us
    all_to_all x1, starting transfers between devices, exchange(): y = lax.all_to_all(x.reshape((DEVS,) + chunk), GROUP, 0, 0, tiled=True)  11.5 us
    all_to_all x1, waiting for transfers between devices, exchange(): y = lax.all_to_all(x.reshape((DEVS,) + chunk), GROUP, 0, 0, tiled=True)  7.21 us
    pallas_call x5, Pallas kernels, call(): pl.pallas_call(kernel, out_shape=tuple((pltpu.VMEM(shape, dtype) for shap...  6.46 us
    pallas_call x1, Pallas kernels, body(): pl.pallas_call(join_kernel, out_shape=jax.ShapeDtypeStruct((ELEMS, LEVELS...  1.29 us
  transfers between devices with their start and end apart: 2, of which 2 were waited for; matrix products, arithmetic and copies ran while one was open for 0% of the time, Pallas kernels for 4%

profile of v5, /device:TPU:1, one launch (start us, length us, event | category | flops | bytes accessed | tf_op | source)
XLA Modules:
  0.0 61.0 jit_solution(18115952584898124358)
XLA Ops:
  0.0 2.2 %pack.1 = (f32[128,128]{1,0:T(8,128)}, s32[8,128]{1,0:T(8,128)S(1)}, f32[32,128]{1,0:T(8,128)S(1)}, f32[8,128]{1,0:T(8,128)S(1)}, f32[8,8,640]{2,1,0:T(8,128)S(1)}) custom-call(s32[1]{0:T(128)} %bitcast.me_ref, s32[8,128]{1,0:T(8,128)} %bitcast.15, s32[8,128]{1,0:T(8,128)} %local_hbm.1, f32[2,8,128]{2,1,0:T(8,128)} %coord_hbm.1, f32[8,128]{1,0:T(8,128)} %mass_hbm.1, ...), custom_call_target="tpu_custom_call" | custom-call | tf_op jit(solution)/shard_map/pack/pallas_call | solution.py:421
  2.2 11.5 %all-to-all-start = ((f32[128,1,128]{2,1,0:T(1,128)}), f32[128,1,128]{2,1,0:T(1,128)S(1)}, u32[]{:S(2)}, u32[]{:S(2)}) async-start(f32[128,1,128]{2,1,0:T(1,128)} %bitcast.3), calls=%async_computation | async-start | bytes 131072 | tf_op jit(solution)/shard_map/all_to_all | solution.py:432
  13.7 2.3 %home.1 = (bf16[640,192]{1,0:T(8,128)(2,1)S(1)}, f32[80,64]{1,0:T(8,128)S(1)}, f32[40,128]{1,0:T(8,128)S(1)}, bf16[1024,256]{1,0:T(8,128)(2,1)S(1)}, s32[8,128]{...) custom-call(f32[8,8,640]{2,1,0:T(8,128)S(1)} %get-tuple-element.27.tracer_ref, ...), custom_call_target="tpu_custom_call" | custom-call | tf_op jit(solution)/shard_map/home/pallas_call | solution.py:421
  15.9 7.2 %all-to-all-done = f32[128,1,128]{2,1,0:T(1,128)S(1)} async-done(((f32[128,1,128]{2,1,0:T(1,128)}), f32[128,1,128]{2,1,0:T(1,128)S(1)}, u32[]{:S(2)}, u32[]{:S(2)}) %all-to-all-start) | async-done | bytes 65568 | tf_op jit(solution)/shard_map/all_to_all | solution.py:432
  23.2 1.3 %serve.1 = (f32[4,128]{1,0:T(4,128)S(1)}, f32[4,128]{1,0:T(4,128)S(1)}, s32[8,128]{1,0:T(8,128)S(1)}, s32[256,128]{1,0:T(8,128)S(1)}, f32[1280,128]{1,0:T(8,128)...) custom-call(s32[1]{0:T(128)} %bitcast.me_ref, f32[128,128]{1,0:T(8,128)S(1)} %bitcast.14, ...), custom_call_target="tpu_custom_call" | custom-call | tf_op jit(solution)/shard_map/serve/pallas_call | solution.py:421
  24.5 0.8 %collective-permute-start = (f32[4,128]{1,0:T(4,128)S(1)}, f32[4,128]{1,0:T(4,128)S(1)}, u32[]{:S(2)}, u32[]{:S(2)}) collective-permute-start(f32[4,128]{1,0:T(4,128)S(1)} %get-tuple-element.38), channel_id=1, source_target_pairs={{0,1},{1,0},{2,3},{3,2},{4,5},{5,4},{6,7},{7,6},{8,9},{9,8},{10,11... | collective-permute-start | bytes 6152 | tf_op jit(solution)/shard_map/ppermute | solution.py:479
  25.2 0.8 %collective-permute-done.got_ref = f32[4,128]{1,0:T(4,128)S(1)} collective-permute-done((f32[4,128]{1,0:T(4,128)S(1)}, f32[4,128]{1,0:T(4,128)S(1)}, u32[]{:S(2)}, u32[]{:S(2)}) %collective-permute-start) | collective-permute-done | bytes 2080 | tf_op jit(solution)/shard_map/ppermute | solution.py:479
  26.1 14.3 %all_to_all.15 = f32[128,4,128]{2,1,0:T(4,128)S(1)} all-to-all(f32[128,4,128]{2,1,0:T(4,128)S(1)} %bitcast.12), channel_id=1, replica_groups=mesh['x'=4,'y'=4,'z'=4,'core'=2] {'core','z','y','x'}, dimensions={0} | all-to-all | bytes 524288 | tf_op jit(solution)/shard_map/all_to_all | solution.py:432
  40.4 0.7 %finish.1 = (f32[1280,128]{1,0:T(8,128)S(1)}, f32[1024,128]{1,0:T(8,128)S(1)}) custom-call(s32[8,128]{1,0:T(8,128)S(1)} %get-tuple-element.36.ids_ref, f32[512,128]{1,0:T(8,128)S(1)} %bitcast.11, s32[256,128]{1,0:T(8,128)S(1)} %get-tuple-element.39.level_ref, f32[1280,128]{1,0:T(8,128)S(1)} %get-tuple-element.40.c_ref, ...), custom_call_target="tpu_custom_call" | custom-call | tf_op jit(solution)/shard_map/finish/pallas_call | solution.py:421
  41.1 18.6 %all_to_all.16 = f32[128,1,1280]{2,1,0:T(1,128)S(1)} all-to-all(f32[128,1,1280]{2,1,0:T(1,128)S(1)} %bitcast.13), channel_id=1, replica_groups=mesh['x'=4,'y'=4,'z'=4,'core'=2] {'core','z','y','x'}, dimensions={0} | all-to-all | bytes 1310720 | tf_op jit(solution)/shard_map/all_to_all | solution.py:432
  59.7 1.3 %join.1 = f32[8,8,640]{2,1,0:T(8,128)} custom-call(s32[8,128]{1,0:T(8,128)S(1)} %get-tuple-element.31.peer_ref, f32[1280,128]{1,0:T(8,128)S(1)} %bitcast.10, bf16[1024,256]{1,0:T(8,128)(2,1)S(1)} %get-tuple-element.47.hot_ref, f32[1024,128]{1,0:T(8,128)S(1)} %get-tuple-element.48.home_ref), custom_call_target="tpu_custom_call" | custom-call | tf_op jit(solution)/shard_map/join/pallas_call | solution.py:491
  (1 shorter events, 0.0 us)
Async XLA Ops:
  2.2 21.0 %all-to-all-start = ((f32[128,1,128]{2,1,0:T(1,128)}), f32[128,1,128]{2,1,0:T(1,128)S(1)}, u32[]{:S(2)}, u32[]{:S(2)}) async-start(f32[128,1,128]{2,1,0:T(1,128)} %bitcast.3), calls=%async_computation | async-start | bytes 131072 | tf_op jit(solution)/shard_map/all_to_all | solution.py:432
  24.5 1.6 %collective-permute-start = (f32[4,128]{1,0:T(4,128)S(1)}, f32[4,128]{1,0:T(4,128)S(1)}, u32[]{:S(2)}, u32[]{:S(2)}) collective-permute-start(f32[4,128]{1,0:T(4,128)S(1)} %get-tuple-element.38), channel_id=1, source_target_pairs={{0,1},{1,0},{2,3},{3,2},{4,5},{5,4},{6,7},{7,6},{8,9},{9,8},{10,11... | collective-permute-start | bytes 6152 | tf_op jit(solution)/shard_map/ppermute | solution.py:479

commit v6 on v5

--- a/solution.py
+++ b/solution.py
@@ -399,10 +399,10 @@
             near = jnp.where(block == p, moved(p), near)
         table.append(jnp.concatenate([near, jnp.where(block == 0, moved(4), 0.0)], axis=1))
     high, mid = split2(jnp.concatenate(table, axis=0))
+    both = jnp.concatenate([high, mid], axis=0)
     for e in range(ELEMS):
-        hot = hot_ref[e * COLS : (e + 1) * COLS, :]
-        at = slice(e * COLS, (e + 1) * COLS)
-        v = dot_nt(hot, high) + dot_nt(hot, mid) + home_ref[at, :Q]
+        picked = dot_nt(hot_ref[e * COLS : (e + 1) * COLS, :], both)
+        v = picked[:, :Q] + picked[:, Q:] + home_ref[e * COLS : (e + 1) * COLS, :Q]
         out_ref[e] = jnp.concatenate([v[8 * k : 8 * k + 8] for k in range(NODES)], axis=1)
         pltpu.make_async_copy(out_ref.at[e], out_hbm.at[e], sem.at[e]).start()
     for e in range(ELEMS):

time: 61.2 us -> 61.2 us (level)
  no operation moved by 1% of the time
where the time goes in v6:
time: 61.2 us; the launch traced here: 61 us
  blocking collectives  33 us (54%)
  starting transfers between devices  12.2 us (20%)
  waiting for transfers between devices  8.03 us (13%)
  Pallas kernels  7.76 us (13%)
    all_to_all x2, blocking collectives, exchange(): y = lax.all_to_all(x.reshape((DEVS,) + chunk), GROUP, 0, 0, tiled=True)  33 us
    all_to_all x1, starting transfers between devices, exchange(): y = lax.all_to_all(x.reshape((DEVS,) + chunk), GROUP, 0, 0, tiled=True)  11.5 us
    all_to_all x1, waiting for transfers between devices, exchange(): y = lax.all_to_all(x.reshape((DEVS,) + chunk), GROUP, 0, 0, tiled=True)  7.21 us
    pallas_call x5, Pallas kernels, call(): pl.pallas_call(kernel, out_shape=tuple((pltpu.VMEM(shape, dtype) for shap...  6.46 us
    pallas_call x1, Pallas kernels, body(): pl.pallas_call(join_kernel, out_shape=jax.ShapeDtypeStruct((ELEMS, LEVELS...  1.3 us
  transfers between devices with their start and end apart: 2, of which 2 were waited for; matrix products, arithmetic and copies ran while one was open for 0% of the time, Pallas kernels for 4%

profile of v6, /device:TPU:1, one launch (start us, length us, event | category | flops | bytes accessed | tf_op | source)
XLA Modules:
  0.0 61.0 jit_solution(12966130227759478163)
XLA Ops:
  0.0 2.2 %pack.1 = (f32[128,128]{1,0:T(8,128)}, s32[8,128]{1,0:T(8,128)S(1)}, f32[32,128]{1,0:T(8,128)S(1)}, f32[8,128]{1,0:T(8,128)S(1)}, f32[8,8,640]{2,1,0:T(8,128)S(1)}) custom-call(s32[1]{0:T(128)} %bitcast.me_ref, s32[8,128]{1,0:T(8,128)} %bitcast.15, s32[8,128]{1,0:T(8,128)} %local_hbm.1, f32[2,8,128]{2,1,0:T(8,128)} %coord_hbm.1, f32[8,128]{1,0:T(8,128)} %mass_hbm.1, ...), custom_call_target="tpu_custom_call" | custom-call | tf_op jit(solution)/shard_map/pack/pallas_call | solution.py:421
  2.2 11.5 %all-to-all-start = ((f32[128,1,128]{2,1,0:T(1,128)}), f32[128,1,128]{2,1,0:T(1,128)S(1)}, u32[]{:S(2)}, u32[]{:S(2)}) async-start(f32[128,1,128]{2,1,0:T(1,128)} %bitcast.3), calls=%async_computation | async-start | bytes 131072 | tf_op jit(solution)/shard_map/all_to_all | solution.py:432
  13.7 2.3 %home.1 = (bf16[640,192]{1,0:T(8,128)(2,1)S(1)}, f32[80,64]{1,0:T(8,128)S(1)}, f32[40,128]{1,0:T(8,128)S(1)}, bf16[1024,256]{1,0:T(8,128)(2,1)S(1)}, s32[8,128]{...) custom-call(f32[8,8,640]{2,1,0:T(8,128)S(1)} %get-tuple-element.27.tracer_ref, ...), custom_call_target="tpu_custom_call" | custom-call | tf_op jit(solution)/shard_map/home/pallas_call | solution.py:421
  15.9 7.2 %all-to-all-done = f32[128,1,128]{2,1,0:T(1,128)S(1)} async-done(((f32[128,1,128]{2,1,0:T(1,128)}), f32[128,1,128]{2,1,0:T(1,128)S(1)}, u32[]{:S(2)}, u32[]{:S(2)}) %all-to-all-start) | async-done | bytes 65568 | tf_op jit(solution)/shard_map/all_to_all | solution.py:432
  23.2 1.3 %serve.1 = (f32[4,128]{1,0:T(4,128)S(1)}, f32[4,128]{1,0:T(4,128)S(1)}, s32[8,128]{1,0:T(8,128)S(1)}, s32[256,128]{1,0:T(8,128)S(1)}, f32[1280,128]{1,0:T(8,128)...) custom-call(s32[1]{0:T(128)} %bitcast.me_ref, f32[128,128]{1,0:T(8,128)S(1)} %bitcast.14, ...), custom_call_target="tpu_custom_call" | custom-call | tf_op jit(solution)/shard_map/serve/pallas_call | solution.py:421
  24.5 0.8 %collective-permute-start = (f32[4,128]{1,0:T(4,128)S(1)}, f32[4,128]{1,0:T(4,128)S(1)}, u32[]{:S(2)}, u32[]{:S(2)}) collective-permute-start(f32[4,128]{1,0:T(4,128)S(1)} %get-tuple-element.38), channel_id=1, source_target_pairs={{0,1},{1,0},{2,3},{3,2},{4,5},{5,4},{6,7},{7,6},{8,9},{9,8},{10,11... | collective-permute-start | bytes 6152 | tf_op jit(solution)/shard_map/ppermute | solution.py:479
  25.2 0.8 %collective-permute-done.got_ref = f32[4,128]{1,0:T(4,128)S(1)} collective-permute-done((f32[4,128]{1,0:T(4,128)S(1)}, f32[4,128]{1,0:T(4,128)S(1)}, u32[]{:S(2)}, u32[]{:S(2)}) %collective-permute-start) | collective-permute-done | bytes 2080 | tf_op jit(solution)/shard_map/ppermute | solution.py:479
  26.1 14.3 %all_to_all.15 = f32[128,4,128]{2,1,0:T(4,128)S(1)} all-to-all(f32[128,4,128]{2,1,0:T(4,128)S(1)} %bitcast.12), channel_id=1, replica_groups=mesh['x'=4,'y'=4,'z'=4,'core'=2] {'core','z','y','x'}, dimensions={0} | all-to-all | bytes 524288 | tf_op jit(solution)/shard_map/all_to_all | solution.py:432
  40.4 0.7 %finish.1 = (f32[1280,128]{1,0:T(8,128)S(1)}, f32[1024,128]{1,0:T(8,128)S(1)}) custom-call(s32[8,128]{1,0:T(8,128)S(1)} %get-tuple-element.36.ids_ref, f32[512,128]{1,0:T(8,128)S(1)} %bitcast.11, s32[256,128]{1,0:T(8,128)S(1)} %get-tuple-element.39.level_ref, f32[1280,128]{1,0:T(8,128)S(1)} %get-tuple-element.40.c_ref, ...), custom_call_target="tpu_custom_call" | custom-call | tf_op jit(solution)/shard_map/finish/pallas_call | solution.py:421
  41.1 18.6 %all_to_all.16 = f32[128,1,1280]{2,1,0:T(1,128)S(1)} all-to-all(f32[128,1,1280]{2,1,0:T(1,128)S(1)} %bitcast.13), channel_id=1, replica_groups=mesh['x'=4,'y'=4,'z'=4,'core'=2] {'core','z','y','x'}, dimensions={0} | all-to-all | bytes 1310720 | tf_op jit(solution)/shard_map/all_to_all | solution.py:432
  59.7 1.3 %join.1 = f32[8,8,640]{2,1,0:T(8,128)} custom-call(s32[8,128]{1,0:T(8,128)S(1)} %get-tuple-element.31.peer_ref, f32[1280,128]{1,0:T(8,128)S(1)} %bitcast.10, bf16[1024,256]{1,0:T(8,128)(2,1)S(1)} %get-tuple-element.47.hot_ref, f32[1024,128]{1,0:T(8,128)S(1)} %get-tuple-element.48.home_ref), custom_call_target="tpu_custom_call" | custom-call | tf_op jit(solution)/shard_map/join/pallas_call | solution.py:491
  (1 shorter events, 0.0 us)
Async XLA Ops:
  2.2 21.0 %all-to-all-start = ((f32[128,1,128]{2,1,0:T(1,128)}), f32[128,1,128]{2,1,0:T(1,128)S(1)}, u32[]{:S(2)}, u32[]{:S(2)}) async-start(f32[128,1,128]{2,1,0:T(1,128)} %bitcast.3), calls=%async_computation | async-start | bytes 131072 | tf_op jit(solution)/shard_map/all_to_all | solution.py:432
  24.5 1.6 %collective-permute-start = (f32[4,128]{1,0:T(4,128)S(1)}, f32[4,128]{1,0:T(4,128)S(1)}, u32[]{:S(2)}, u32[]{:S(2)}) collective-permute-start(f32[4,128]{1,0:T(4,128)S(1)} %get-tuple-element.38), channel_id=1, source_target_pairs={{0,1},{1,0},{2,3},{3,2},{4,5},{5,4},{6,7},{7,6},{8,9},{9,8},{10,11... | collective-permute-start | bytes 6152 | tf_op jit(solution)/shard_map/ppermute | solution.py:479

commit v7 on v6

--- a/solution.py
+++ b/solution.py
@@ -399,12 +399,13 @@
             near = jnp.where(block == p, moved(p), near)
         table.append(jnp.concatenate([near, jnp.where(block == 0, moved(4), 0.0)], axis=1))
     high, mid = split2(jnp.concatenate(table, axis=0))
-    both = jnp.concatenate([high, mid], axis=0)
-    for e in range(ELEMS):
-        picked = dot_nt(hot_ref[e * COLS : (e + 1) * COLS, :], both)
-        v = picked[:, :Q] + picked[:, Q:] + home_ref[e * COLS : (e + 1) * COLS, :Q]
-        out_ref[e] = jnp.concatenate([v[8 * k : 8 * k + 8] for k in range(NODES)], axis=1)
-        pltpu.make_async_copy(out_ref.at[e], out_hbm.at[e], sem.at[e]).start()
+    for e0 in range(0, ELEMS, 2):
+        hot = hot_ref[e0 * COLS : (e0 + 2) * COLS, :]
+        picked = dot_nt(hot, high) + dot_nt(hot, mid)
+        for e in range(e0, e0 + 2):
+            v = picked[(e - e0) * COLS : (e - e0 + 1) * COLS] + home_ref[e * COLS : (e + 1) * COLS, :Q]
+            out_ref[e] = jnp.concatenate([v[8 * k : 8 * k + 8] for k in range(NODES)], axis=1)
+            pltpu.make_async_copy(out_ref.at[e], out_hbm.at[e], sem.at[e]).start()
     for e in range(ELEMS):
         pltpu.make_async_copy(out_ref.at[e], out_hbm.at[e], sem.at[e]).wait()
 

time: 61.2 us -> 61.2 us (level)
  no operation moved by 1% of the time
where the time goes in v7:
time: 61.2 us; the launch traced here: 61 us
  blocking collectives  33 us (54%)
  starting transfers between devices  12.2 us (20%)
  waiting for transfers between devices  8.03 us (13%)
  Pallas kernels  7.75 us (13%)
    all_to_all x2, blocking collectives, exchange(): y = lax.all_to_all(x.reshape((DEVS,) + chunk), GROUP, 0, 0, tiled=True)  33 us
    all_to_all x1, starting transfers between devices, exchange(): y = lax.all_to_all(x.reshape((DEVS,) + chunk), GROUP, 0, 0, tiled=True)  11.5 us
    all_to_all x1, waiting for transfers between devices, exchange(): y = lax.all_to_all(x.reshape((DEVS,) + chunk), GROUP, 0, 0, tiled=True)  7.21 us
    pallas_call x5, Pallas kernels, call(): pl.pallas_call(kernel, out_shape=tuple((pltpu.VMEM(shape, dtype) for shap...  6.46 us
    pallas_call x1, Pallas kernels, body(): pl.pallas_call(join_kernel, out_shape=jax.ShapeDtypeStruct((ELEMS, LEVELS...  1.29 us
  transfers between devices with their start and end apart: 2, of which 2 were waited for; matrix products, arithmetic and copies ran while one was open for 0% of the time, Pallas kernels for 4%

profile of v7, /device:TPU:1, one launch (start us, length us, event | category | flops | bytes accessed | tf_op | source)
XLA Modules:
  0.0 61.0 jit_solution(12237667233055011623)
XLA Ops:
  0.0 2.2 %pack.1 = (f32[128,128]{1,0:T(8,128)}, s32[8,128]{1,0:T(8,128)S(1)}, f32[32,128]{1,0:T(8,128)S(1)}, f32[8,128]{1,0:T(8,128)S(1)}, f32[8,8,640]{2,1,0:T(8,128)S(1)}) custom-call(s32[1]{0:T(128)} %bitcast.me_ref, s32[8,128]{1,0:T(8,128)} %bitcast.15, s32[8,128]{1,0:T(8,128)} %local_hbm.1, f32[2,8,128]{2,1,0:T(8,128)} %coord_hbm.1, f32[8,128]{1,0:T(8,128)} %mass_hbm.1, ...), custom_call_target="tpu_custom_call" | custom-call | tf_op jit(solution)/shard_map/pack/pallas_call | solution.py:422
  2.2 11.5 %all-to-all-start = ((f32[128,1,128]{2,1,0:T(1,128)}), f32[128,1,128]{2,1,0:T(1,128)S(1)}, u32[]{:S(2)}, u32[]{:S(2)}) async-start(f32[128,1,128]{2,1,0:T(1,128)} %bitcast.3), calls=%async_computation | async-start | bytes 131072 | tf_op jit(solution)/shard_map/all_to_all | solution.py:433
  13.7 2.3 %home.1 = (bf16[640,192]{1,0:T(8,128)(2,1)S(1)}, f32[80,64]{1,0:T(8,128)S(1)}, f32[40,128]{1,0:T(8,128)S(1)}, bf16[1024,256]{1,0:T(8,128)(2,1)S(1)}, s32[8,128]{...) custom-call(f32[8,8,640]{2,1,0:T(8,128)S(1)} %get-tuple-element.27.tracer_ref, ...), custom_call_target="tpu_custom_call" | custom-call | tf_op jit(solution)/shard_map/home/pallas_call | solution.py:422
  15.9 7.2 %all-to-all-done = f32[128,1,128]{2,1,0:T(1,128)S(1)} async-done(((f32[128,1,128]{2,1,0:T(1,128)}), f32[128,1,128]{2,1,0:T(1,128)S(1)}, u32[]{:S(2)}, u32[]{:S(2)}) %all-to-all-start) | async-done | bytes 65568 | tf_op jit(solution)/shard_map/all_to_all | solution.py:433
  23.2 1.3 %serve.1 = (f32[4,128]{1,0:T(4,128)S(1)}, f32[4,128]{1,0:T(4,128)S(1)}, s32[8,128]{1,0:T(8,128)S(1)}, s32[256,128]{1,0:T(8,128)S(1)}, f32[1280,128]{1,0:T(8,128)...) custom-call(s32[1]{0:T(128)} %bitcast.me_ref, f32[128,128]{1,0:T(8,128)S(1)} %bitcast.14, ...), custom_call_target="tpu_custom_call" | custom-call | tf_op jit(solution)/shard_map/serve/pallas_call | solution.py:422
  24.5 0.8 %collective-permute-start = (f32[4,128]{1,0:T(4,128)S(1)}, f32[4,128]{1,0:T(4,128)S(1)}, u32[]{:S(2)}, u32[]{:S(2)}) collective-permute-start(f32[4,128]{1,0:T(4,128)S(1)} %get-tuple-element.38), channel_id=1, source_target_pairs={{0,1},{1,0},{2,3},{3,2},{4,5},{5,4},{6,7},{7,6},{8,9},{9,8},{10,11... | collective-permute-start | bytes 6152 | tf_op jit(solution)/shard_map/ppermute | solution.py:480
  25.2 0.8 %collective-permute-done.got_ref = f32[4,128]{1,0:T(4,128)S(1)} collective-permute-done((f32[4,128]{1,0:T(4,128)S(1)}, f32[4,128]{1,0:T(4,128)S(1)}, u32[]{:S(2)}, u32[]{:S(2)}) %collective-permute-start) | collective-permute-done | bytes 2080 | tf_op jit(solution)/shard_map/ppermute | solution.py:480
  26.1 14.3 %all_to_all.15 = f32[128,4,128]{2,1,0:T(4,128)S(1)} all-to-all(f32[128,4,128]{2,1,0:T(4,128)S(1)} %bitcast.12), channel_id=1, replica_groups=mesh['x'=4,'y'=4,'z'=4,'core'=2] {'core','z','y','x'}, dimensions={0} | all-to-all | bytes 524288 | tf_op jit(solution)/shard_map/all_to_all | solution.py:433
  40.4 0.7 %finish.1 = (f32[1280,128]{1,0:T(8,128)S(1)}, f32[1024,128]{1,0:T(8,128)S(1)}) custom-call(s32[8,128]{1,0:T(8,128)S(1)} %get-tuple-element.36.ids_ref, f32[512,128]{1,0:T(8,128)S(1)} %bitcast.11, s32[256,128]{1,0:T(8,128)S(1)} %get-tuple-element.39.level_ref, f32[1280,128]{1,0:T(8,128)S(1)} %get-tuple-element.40.c_ref, ...), custom_call_target="tpu_custom_call" | custom-call | tf_op jit(solution)/shard_map/finish/pallas_call | solution.py:422
  41.1 18.6 %all_to_all.16 = f32[128,1,1280]{2,1,0:T(1,128)S(1)} all-to-all(f32[128,1,1280]{2,1,0:T(1,128)S(1)} %bitcast.13), channel_id=1, replica_groups=mesh['x'=4,'y'=4,'z'=4,'core'=2] {'core','z','y','x'}, dimensions={0} | all-to-all | bytes 1310720 | tf_op jit(solution)/shard_map/all_to_all | solution.py:433
  59.7 1.3 %join.1 = f32[8,8,640]{2,1,0:T(8,128)} custom-call(s32[8,128]{1,0:T(8,128)S(1)} %get-tuple-element.31.peer_ref, f32[1280,128]{1,0:T(8,128)S(1)} %bitcast.10, bf16[1024,256]{1,0:T(8,128)(2,1)S(1)} %get-tuple-element.47.hot_ref, f32[1024,128]{1,0:T(8,128)S(1)} %get-tuple-element.48.home_ref), custom_call_target="tpu_custom_call" | custom-call | tf_op jit(solution)/shard_map/join/pallas_call | solution.py:492
  (1 shorter events, 0.0 us)
Async XLA Ops:
  2.2 21.0 %all-to-all-start = ((f32[128,1,128]{2,1,0:T(1,128)}), f32[128,1,128]{2,1,0:T(1,128)S(1)}, u32[]{:S(2)}, u32[]{:S(2)}) async-start(f32[128,1,128]{2,1,0:T(1,128)} %bitcast.3), calls=%async_computation | async-start | bytes 131072 | tf_op jit(solution)/shard_map/all_to_all | solution.py:433
  24.5 1.6 %collective-permute-start = (f32[4,128]{1,0:T(4,128)S(1)}, f32[4,128]{1,0:T(4,128)S(1)}, u32[]{:S(2)}, u32[]{:S(2)}) collective-permute-start(f32[4,128]{1,0:T(4,128)S(1)} %get-tuple-element.38), channel_id=1, source_target_pairs={{0,1},{1,0},{2,3},{3,2},{4,5},{5,4},{6,7},{7,6},{8,9},{9,8},{10,11... | collective-permute-start | bytes 6152 | tf_op jit(solution)/shard_map/ppermute | solution.py:480
